TPU v7x, 512 devices: a whole 4x8x8 slice. The times are simulated.
512 devices in a mesh: graph: 128 (over z, y, core), member: 4 (over x).
Axes of the slice: x: 4, y: 8, z: 8, core: 2. Of those that a mesh axis runs over, the one named last changes fastest.
Arguments:
- node_latents: bfloat16 [16, 16384, 512], P('member', 'graph'), may hold values from -6 to 6
- edge_latents: bfloat16 [98304, 512], P('graph'), may hold values from -6 to 6
- neighbours: int32 [128, 4], P('graph'), may hold values from 0 to 127, as said below
- edge_source: int32 [128, 768], P('graph'), may hold values from 0 to 639, as said below
- edge_dest: int32 [128, 768], P('graph'), may hold values from 0 to 127, as said below
- edge_count: int32 [128], P('graph'), may hold values from 153 to 768, as said below
- edge_in: bfloat16 [1, 3, 512, 512], replicated, may hold values from -0.15625 to 0.15625
- edge_out: bfloat16 [1, 512, 512], replicated, may hold values from -0.25 to 0.25
- node_in: bfloat16 [1, 2, 512, 512], replicated, may hold values from -0.1875 to 0.1875
- node_out: bfloat16 [1, 512, 512], replicated, may hold values from -0.25 to 0.25
- biases: float32 [1, 4, 512], replicated, may hold values from -3 to 3
- gains: float32 [1, 2, 512], replicated, may hold values from 0.25 to 1.75
Outputs:
- ens_mean: bfloat16 [16384, 512], P('graph')
- ens_spread: bfloat16 [16384, 512], P('graph')
Inputs may be any that keep to these rules, and one draw needn't show every extreme that they name: `neighbours`: row b lists 4 distinct blocks other than b, each within 3 blocks of b along the closed order of blocks (numbers taken modulo 128). `edge_source`: among the live edge slots of one block, at most 32 distinct sender nodes lie in any one listed block, and exactly 32 in one of them. `edge_dest`: every node receives at least one live edge slot of its block. `edge_count`: some block has all 768 slots live.
All inputs are finite; a program needn't handle non-finite values.
Results may differ from a plain program's by a relative error of at most 0.006.
Values may be sent and summed in bfloat16 or wider, within the bound.
A program may use at most 64 MiB of HBM per device.

v0:
```python
import jax
import jax.numpy as jnp
from jax import lax
from jax.sharding import PartitionSpec as P

RADIUS = 3


def from_behind(value, axis, steps):
    count = lax.axis_size(axis)
    pairs = [(source, (source + steps) % count) for source in range(count)]
    return lax.ppermute(value, axis, pairs)


def copy_for_each(shard, axis):
    copies = jnp.broadcast_to(shard, (lax.axis_size(axis), *shard.shape))
    return lax.all_to_all(copies, axis, split_axis=0, concat_axis=0, tiled=True)


def taken_together(shard, axis):
    everything = copy_for_each(shard, axis)
    return jnp.sum(everything, axis=0)


def together(arrays, axis):
    ends = [0]
    for a in arrays:
        ends.append(ends[-1] + a.size)
    total = taken_together(jnp.concatenate([a.ravel() for a in arrays]), axis)
    return tuple((total[b:e].reshape(a.shape) for a, b, e in zip(arrays, ends, ends[1:])))


def layer_norm(values, gain):
    centre = jnp.mean(values, axis=-1, keepdims=True)
    centered = values - centre
    variance = jnp.mean(centered * centered, axis=-1, keepdims=True)
    return centered * lax.rsqrt(variance + 1e-05) * gain


def fetch_block(sender_proj, offset):
    return from_behind(sender_proj, "graph", offset)


def edge_update(
    state_rows, sender_rows, dest_rows, dest_hot, weight_in, weight_out, bias_rows, gain
):
    edge_proj = jnp.dot(state_rows, weight_in, preferred_element_type=jnp.float32)[None]
    hidden = edge_proj + sender_rows.astype(jnp.float32) + dest_rows + bias_rows[0]
    activated = jax.nn.silu(hidden).astype(jnp.bfloat16)
    mixed = (
        jnp.einsum("mel,lk->mek", activated, weight_out, preferred_element_type=jnp.float32)
        + bias_rows[1]
    )
    updated = (state_rows.astype(jnp.float32) + layer_norm(mixed, gain)).astype(jnp.bfloat16)
    partial_sum = jnp.einsum("en,mel->mnl", dest_hot, updated, preferred_element_type=jnp.float32)
    return (updated, partial_sum)


def local(
    node_latents,
    edge_latents,
    neighbours,
    edge_source,
    edge_dest,
    edge_count,
    edge_in,
    edge_out,
    node_in,
    node_out,
    biases,
    gains,
):
    members, block_rows, latent_width = node_latents.shape
    edge_slots = edge_source.shape[1]
    nbr_count = neighbours.shape[1]
    groups = lax.axis_size("graph")
    own_index = lax.axis_index("graph")
    offsets = [reach_by for reach_by in range(1, RADIUS + 1)] + [
        -reach_by for reach_by in range(1, RADIUS + 1)
    ]
    src_slot = edge_source[0] // block_rows
    src_node = edge_source[0] % block_rows
    dst_node = edge_dest[0]
    is_live = jnp.arange(edge_slots, dtype=jnp.int32) < edge_count[0]
    distance = (own_index - neighbours[0]) % groups
    signed = jnp.where(distance > groups // 2, distance - groups, distance)
    position = jnp.where(signed > 0, signed - 1, RADIUS - signed - 1)
    slot_ids = jnp.arange(nbr_count, dtype=jnp.int32)
    slot_match = src_slot[:, None] == slot_ids[None, :]
    slot_position = jnp.sum(jnp.where(slot_match, position[None, :], 0), axis=1)
    is_own = src_slot == nbr_count
    node_ids = jnp.arange(block_rows, dtype=jnp.int32)
    row_index = jnp.where(is_own, src_node, block_rows * (1 + slot_position) + src_node)
    dest_hot = ((dst_node[:, None] == node_ids[None, :]) & is_live[:, None]).astype(jnp.bfloat16)
    edge_state = edge_latents
    state = node_latents
    edge_weights = edge_in[0]
    sender_proj = jnp.einsum(
        "mnl,lk->mnk", state, edge_weights[1], preferred_element_type=jnp.float32
    ).astype(jnp.bfloat16)
    receiver_proj = jnp.einsum(
        "mnl,lk->mnk", state, edge_weights[2], preferred_element_type=jnp.float32
    )
    pieces = [sender_proj] + [fetch_block(sender_proj, reach_by) for reach_by in offsets]
    row_table = jnp.concatenate(pieces, axis=1)
    senders = jnp.take(row_table, row_index, axis=1)
    dest_proj = jnp.take(receiver_proj, dst_node, axis=1)
    edge_state, total = edge_update(
        edge_state,
        senders,
        dest_proj,
        dest_hot,
        edge_weights[0],
        edge_out[0],
        biases[0],
        gains[0, 0],
    )
    gathered = total.astype(jnp.bfloat16)
    node_weights = node_in[0]
    node_hidden = jnp.einsum(
        "mnl,lk->mnk", state, node_weights[0], preferred_element_type=jnp.float32
    )
    node_hidden = (
        node_hidden
        + jnp.einsum("mnl,lk->mnk", gathered, node_weights[1], preferred_element_type=jnp.float32)
        + biases[0, 2]
    )
    node_act = jax.nn.silu(node_hidden).astype(jnp.bfloat16)
    node_mixed = (
        jnp.einsum("mnl,lk->mnk", node_act, node_out[0], preferred_element_type=jnp.float32)
        + biases[0, 3]
    )
    state = (state.astype(jnp.float32) + layer_norm(node_mixed, gains[0, 1])).astype(jnp.bfloat16)
    finals = state.astype(jnp.float32)
    ensemble = members * lax.axis_size("member")
    total_state, squares = together(
        (jnp.sum(finals, axis=0), jnp.sum(finals * finals, axis=0)), "member"
    )
    centre = total_state / ensemble
    spread = jnp.sqrt(squares / ensemble - centre * centre)
    return (centre.astype(jnp.bfloat16), spread.astype(jnp.bfloat16))


def solution(mesh):
    return jax.shard_map(
        local,
        mesh=mesh,
        in_specs=(
            P("member", "graph", None),
            P("graph", None),
            P("graph", None),
            P("graph", None),
            P("graph", None),
            P("graph"),
            P(),
            P(),
            P(),
            P(),
            P(),
            P(),
        ),
        out_specs=(P("graph", None), P("graph", None)),
        check_vma=False,
    )
```

profile of v0, /device:TPU:2, one launch (start us, length us, event | category | flops | bytes accessed | tf_op | source)
XLA Modules:
  0.0 129.7 jit_solution(3281422372189918436)
XLA Ops:
  0.6 0.0 copy-start
  0.6 0.0 copy-start.1
  0.7 0.0 copy-start.7
  0.7 0.0 copy-start.10
  0.7 0.0 copy-start.6
  0.7 0.0 copy-start.8
  0.7 0.0 copy-start.2
  0.7 2.7 %constant_dynamic-update-slice_fusion.6 = (bf16[4,896,512]{2,1,0:T(8,128)(2,1)}, bf16[4,128,512]{2,1,0:T(8,128)(2,1)}) fusion(bf16[4,128,512]{2,1,0:T(8,128)(2,1)} %param.12, bf16[1,3,512,512]{3,2,1,0:T(8,128)(2,1)} %param.18), kind=kOutput, calls=%fused_computation.67 | convolution fusion | flops 268697600 | bytes 2097152 | tf_op jit(solution)/shard_map/mnl,lk->mnk/dot_general | solution.py:98
  3.4 0.0 copy-start.9
  3.4 2.0 %collective-permute-start = (bf16[4,128,512]{2,1,0:T(8,128)(2,1)}, bf16[4,128,512]{2,1,0:T(8,128)(2,1)}, u32[]{:S(2)}, u32[]{:S(2)}) collective-permute-start(bf16[4,128,512]{2,1,0:T(8,128)(2,1)} %get-tuple-element.13), channel_id=1, source_target_pairs={{0,4},{4,8},{8,12},{12,16},{16,20},{20,24},{24,28},{28,32},{32,36}... | collective-permute-start | bytes 1572872 | tf_op jit(solution)/shard_map/ppermute | solution.py:12
  5.5 3.5 %collective-permute-start.1 = (bf16[4,128,512]{2,1,0:T(8,128)(2,1)}, bf16[4,128,512]{2,1,0:T(8,128)(2,1)}, u32[]{:S(2)}, u32[]{:S(2)}) collective-permute-start(bf16[4,128,512]{2,1,0:T(8,128)(2,1)} %get-tuple-element.13), channel_id=1, source_target_pairs={{0,8},{4,12},{8,16},{12,20},{16,24},{20,28},{24,32},{28,36},{32,40... | collective-permute-start | bytes 1572872 | tf_op jit(solution)/shard_map/ppermute | solution.py:12
  9.0 4.5 %collective-permute-start.2 = (bf16[4,128,512]{2,1,0:T(8,128)(2,1)}, bf16[4,128,512]{2,1,0:T(8,128)(2,1)}, u32[]{:S(2)}, u32[]{:S(2)}) collective-permute-start(bf16[4,128,512]{2,1,0:T(8,128)(2,1)} %get-tuple-element.13), channel_id=1, source_target_pairs={{0,12},{4,16},{8,20},{12,24},{16,28},{20,32},{24,36},{28,40},{32,4... | collective-permute-start | bytes 1572872 | tf_op jit(solution)/shard_map/ppermute | solution.py:12
  13.5 9.2 %collective-permute-start.3 = (bf16[4,128,512]{2,1,0:T(8,128)(2,1)}, bf16[4,128,512]{2,1,0:T(8,128)(2,1)}, u32[]{:S(2)}, u32[]{:S(2)}) collective-permute-start(bf16[4,128,512]{2,1,0:T(8,128)(2,1)} %get-tuple-element.13), channel_id=1, source_target_pairs={{0,508},{4,0},{8,4},{12,8},{16,12},{20,16},{24,20},{28,24},{32,28}... | collective-permute-start | bytes 1572872 | tf_op jit(solution)/shard_map/ppermute | solution.py:12
  22.7 4.2 %collective-permute-start.4 = (bf16[4,128,512]{2,1,0:T(8,128)(2,1)}, bf16[4,128,512]{2,1,0:T(8,128)(2,1)}, u32[]{:S(2)}, u32[]{:S(2)}) collective-permute-start(bf16[4,128,512]{2,1,0:T(8,128)(2,1)} %get-tuple-element.13), channel_id=1, source_target_pairs={{0,504},{4,508},{8,0},{12,4},{16,8},{20,12},{24,16},{28,20},{32,24... | collective-permute-start | bytes 1572872 | tf_op jit(solution)/shard_map/ppermute | solution.py:12
  26.9 1.6 %fusion.17 = f32[4,128,512]{2,1,0:T(8,128)S(1)} fusion(bf16[4,128,512]{2,1,0:T(8,128)(2,1)} %param.12, bf16[1,3,512,512]{3,2,1,0:T(8,128)(2,1)} %param.18), kind=kOutput, calls=%fused_computation.33 | convolution fusion | flops 268435456 | bytes 2097152 | tf_op jit(solution)/shard_map/mnl,lk->mnk/dot_general | solution.py:101
  28.5 0.0 copy-done.7
  28.6 0.0 copy-done.10
  28.6 0.1 select_reduce_fusion
  28.7 0.0 copy-done.6
  28.7 0.0 copy-done.8
  28.8 0.0 copy-done.2
  28.8 2.8 %fusion.23 = f32[768,512]{1,0:T(8,128)} fusion(bf16[768,512]{1,0:T(8,128)(2,1)S(1)} %copy-done.2, bf16[1,3,512,512]{3,2,1,0:T(8,128)(2,1)} %param.18), kind=kOutput, calls=%fused_computation.39 | convolution fusion | flops 402653184 | bytes 2883584 | tf_op jit(solution)/shard_map/dot_general | solution.py:47
  31.6 0.0 copy-done.1
  31.6 2.5 %fusion.20 = f32[4,128,512]{2,1,0:T(8,128)} fusion(bf16[4,128,512]{2,1,0:T(8,128)(2,1)S(1)} %copy-done.1, bf16[1,2,512,512]{3,2,1,0:T(8,128)(2,1)} %param.20), kind=kOutput, calls=%fused_computation.36 | convolution fusion | flops 268435456 | bytes 2097152 | tf_op jit(solution)/shard_map/mnl,lk->mnk/dot_general | solution.py:120
  34.0 0.0 copy-done.9
  34.8 1.4 %copy.34 = f32[768,512]{0,1:T(8,128)} copy(bf16[768,512]{1,0:T(8,128)(2,1)S(1)} %copy-done.2) | data formatting | bytes 2359296 | tf_op jit(solution)/shard_map/convert_element_type | solution.py:54
  36.2 0.7 copy.37
  36.9 6.0 %gather_fusion.1 = f32[768,4,512]{2,1,0:T(4,128)} fusion(f32[4,128,512]{2,0,1:T(4,128)S(1)} %copy.37, s32[1024]{0:T(1024)S(1)} %get-tuple-element.18), kind=kCustom, calls=%fused_computation.1 | custom fusion | bytes 12585984 | tf_op jit(solution)/shard_map/jit(_take)/gather | solution.py:107
  42.9 0.0 collective-permute-done
  42.9 3.2 %collective-permute-start.5 = (bf16[4,128,512]{2,1,0:T(8,128)(2,1)}, bf16[4,128,512]{2,1,0:T(8,128)(2,1)S(1)}, u32[]{:S(2)}, u32[]{:S(2)}) collective-permute-start(bf16[4,128,512]{2,1,0:T(8,128)(2,1)} %get-tuple-element.13), channel_id=1, source_target_pairs={{0,500},{4,504},{8,508},{12,0},{16,4},{20,8},{24,12},{28,16},{32,2... | collective-permute-start | bytes 1572872 | tf_op jit(solution)/shard_map/ppermute | solution.py:12
  46.1 1.9 %constant_dynamic-update-slice_fusion.5 = bf16[4,896,512]{2,1,0:T(8,128)(2,1)} fusion(bf16[4,896,512]{2,1,0:T(8,128)(2,1)} %get-tuple-element.12, bf16[4,128,512]{2,1,0:T(8,128)(2,1)} %collective-permute-done), kind=kLoop, calls=%fused_computation.66 | loop fusion | bytes 1048576
  48.0 0.0 collective-permute-done.1
  48.0 1.9 %constant_dynamic-update-slice_fusion.4 = bf16[4,896,512]{2,1,0:T(8,128)(2,1)} fusion(bf16[4,896,512]{2,1,0:T(8,128)(2,1)} %constant_dynamic-update-slice_fusion.5, bf16[4,128,512]{2,1,0:T(8,128)(2,1)} %collective-permute-done.1), kind=kLoop, calls=%fused_computation.65 | loop fusion | bytes 1048576
  49.9 1.2 collective-permute-done.2
  51.2 1.9 %constant_dynamic-update-slice_fusion.3 = bf16[4,896,512]{2,1,0:T(8,128)(2,1)} fusion(bf16[4,896,512]{2,1,0:T(8,128)(2,1)} %constant_dynamic-update-slice_fusion.4, bf16[4,128,512]{2,1,0:T(8,128)(2,1)} %collective-permute-done.2), kind=kLoop, calls=%fused_computation.64 | loop fusion | bytes 1048576
  53.0 0.0 collective-permute-done.3
  53.0 1.9 %constant_dynamic-update-slice_fusion.2 = bf16[4,896,512]{2,1,0:T(8,128)(2,1)} fusion(bf16[4,896,512]{2,1,0:T(8,128)(2,1)} %constant_dynamic-update-slice_fusion.3, bf16[4,128,512]{2,1,0:T(8,128)(2,1)} %collective-permute-done.3), kind=kLoop, calls=%fused_computation.63 | loop fusion | bytes 1048576
  54.9 0.0 collective-permute-done.4
  54.9 1.9 %constant_dynamic-update-slice_fusion.1 = bf16[4,896,512]{2,1,0:T(8,128)(2,1)} fusion(bf16[4,896,512]{2,1,0:T(8,128)(2,1)} %constant_dynamic-update-slice_fusion.2, bf16[4,128,512]{2,1,0:T(8,128)(2,1)} %collective-permute-done.4), kind=kLoop, calls=%fused_computation.62 | loop fusion | bytes 1048576
  56.8 7.9 %collective-permute-done.5 = bf16[4,128,512]{2,1,0:T(8,128)(2,1)S(1)} collective-permute-done((bf16[4,128,512]{2,1,0:T(8,128)(2,1)}, bf16[4,128,512]{2,1,0:T(8,128)(2,1)S(1)}, u32[]{:S(2)}, u32[]{:S(2)}) %collective-permute-start.5) | collective-permute-done | bytes 524320 | tf_op jit(solution)/shard_map/ppermute | solution.py:12
  64.6 0.8 constant_dynamic-update-slice_fusion
  65.5 6.8 %copy.35 = bf16[4,896,512]{2,0,1:T(4,128)(2,1)} copy(bf16[4,896,512]{2,1,0:T(8,128)(2,1)} %constant_dynamic-update-slice_fusion) | data formatting | bytes 7340032 | tf_op jit(solution)/shard_map/concatenate | solution.py:105
  72.3 0.0 copy-start.4
  72.3 8.5 %gather_fusion = bf16[768,4,512]{2,1,0:T(4,128)(2,1)} fusion(bf16[4,896,512]{2,0,1:T(4,128)(2,1)} %copy.35, s32[1024]{0:T(1024)S(1)} %get-tuple-element.19), kind=kCustom, calls=%fused_computation | custom fusion | bytes 6294528 | tf_op jit(solution)/shard_map/jit(_take)/gather | solution.py:106
  80.7 0.0 copy-done
  80.7 0.0 copy-done.4
  80.7 8.1 %add_reduce_fusion = (f32[4,768]{1,0:T(4,128)S(1)}, f32[4,768,512]{1,2,0:T(8,128)S(1)}) fusion(f32[512]{0:T(512)S(1)} %bitcast.98, bf16[1,512,512]{2,1,0:T(8,128)(2,1)S(1)} %copy-done, f32[768,4,512]{2,1,0:T(4,128)} %gather_fusion.1, bf16[768,4,512]{2,1,0:T(4,128)(2,1)} %gather_fusion, f32[512]{0:T(512)S(1)} %bitcast.104, f32[768,512]{1,0:T(8,128)S(1)} %copy-done.4, ...), kind=kOutput, calls=%fused_computation.13 | convolution fusion | flops 1631056896 | bytes 17843712 | tf_op jit(solution)/shard_map/mel,lk->mek/dot_general | solution.py:51
  88.9 0.0 copy-start.3
  88.9 0.9 multiply_reduce_fusion
  89.8 0.4 copy-done.3
  90.3 0.0 copy-start.5
  90.3 2.7 %fusion.12 = bf16[4,128,512]{1,2,0:T(8,128)(2,1)} fusion(f32[4,768,512]{1,2,0:T(8,128)S(1)} %get-tuple-element.15, f32[512]{0:T(512)S(1)} %bitcast.101, f32[4,768]{1,0:T(4,128)S(1)} %add_rsqrt_fusion, f32[4,768]{1,0:T(4,128)S(1)} %broadcast_multiply_fusion, f32[512]{0:T(512)S(1)} %bitcast.100, f32[768,512]{0,1:T(8,128)S(1)} %copy-done.3, ...), kind=kOutput, calls=%fused_computation.25 | convolution fusion | flops 412549120 | bytes 8421120 | tf_op jit(solution)/shard_map/en,mel->mnl/dot_general | solution.py:55
  92.9 0.0 copy-done.5
  92.9 2.3 %fusion.54 = (f32[4,128]{1,0:T(4,128)S(1)}, f32[4,128,512]{2,1,0:T(8,128)S(1)}) fusion(f32[512]{0:T(512)S(1)} %bitcast.103, bf16[1,512,512]{2,1,0:T(8,128)(2,1)} %param.21, f32[4,128,512]{2,1,0:T(8,128)S(1)} %copy-done.5, bf16[4,128,512]{1,2,0:T(8,128)(2,1)} %fusion.12, f32[512]{0:T(512)S(1)} %bitcast.102, bf16[1,2,512,512]{3,2,1,0:T(8,128)(2,1)} %param.20), kind=kOutput, calls=%fused_computation.113 | convolution fusion | flops 539229696 | bytes 3676160 | tf_op jit(solution)/shard_map/mnl,lk->mnk/dot_general | solution.py:130
  95.3 0.3 multiply_reduce_fusion.1
  95.6 0.3 convert_reduce_fusion
  95.9 0.1 copy.48
  96.0 0.1 copy.49
  96.1 1.1 broadcast_in_dim.55
  97.2 28.9 %all_to_all.6 = f32[4,1,131072]{2,1,0:T(1,128)S(1)} all-to-all(f32[4,1,131072]{2,1,0:T(1,128)S(1)} %broadcast_in_dim.55), channel_id=1, replica_groups=mesh['graph'=128,'member'=4] {'member'}, dimensions={0} | all-to-all | bytes 4194304 | tf_op jit(solution)/shard_map/all_to_all | solution.py:17
  126.1 1.9 %reduce_sum.79 = f32[131072]{0:T(1024)S(1)} reduce(f32[4,1,131072]{2,1,0:T(1,128)S(1)} %all_to_all.6, f32[]{:T(128)} %constant.106.clone.1), dimensions={0,1}, to_apply=%region_7.8 | reduce | flops 393216 | bytes 2621444 | tf_op jit(solution)/shard_map/reduce_sum | solution.py:22
  128.1 0.1 fusion.38
  128.2 0.7 convert_element_type.53
  128.9 0.7 sqrt.7
  (17 shorter events, 0.2 us)
Async XLA Ops:
  0.6 80.1 %copy-start = (bf16[1,512,512]{2,1,0:T(8,128)(2,1)S(1)}, bf16[1,512,512]{2,1,0:T(8,128)(2,1)}, u32[]{:S(2)}) copy-start(bf16[1,512,512]{2,1,0:T(8,128)(2,1)} %param.19) | copy-start | bytes 1572868
  0.6 30.9 %copy-start.1 = (bf16[4,128,512]{2,1,0:T(8,128)(2,1)S(1)}, bf16[4,128,512]{2,1,0:T(8,128)(2,1)}, u32[]{:S(2)}) copy-start(bf16[4,128,512]{2,1,0:T(8,128)(2,1)} %param.12) | copy-start | bytes 1572868
  0.7 27.8 %copy-start.7 = (s32[1,768]{1,0:T(1,128)S(1)}, s32[1,768]{1,0:T(1,128)}, u32[]{:S(2)}) copy-start(s32[1,768]{1,0:T(1,128)} %param.15) | copy-start | bytes 9220
  0.7 27.9 %copy-start.10 = (s32[1,4]{1,0:T(1,128)S(1)}, s32[1,4]{1,0:T(1,128)}, u32[]{:S(2)}) copy-start(s32[1,4]{1,0:T(1,128)} %param.14) | copy-start | bytes 52
  0.7 28.0 %copy-start.6 = (s32[1,768]{1,0:T(1,128)S(1)}, s32[1,768]{1,0:T(1,128)}, u32[]{:S(2)}) copy-start(s32[1,768]{1,0:T(1,128)} %param.16) | copy-start | bytes 9220
  0.7 28.0 %copy-start.8 = (f32[1,4,512]{2,1,0:T(4,128)S(1)}, f32[1,4,512]{2,1,0:T(4,128)}, u32[]{:S(2)}) copy-start(f32[1,4,512]{2,1,0:T(4,128)} %param.22) | copy-start | bytes 24580
  0.7 28.1 %copy-start.2 = (bf16[768,512]{1,0:T(8,128)(2,1)S(1)}, bf16[768,512]{1,0:T(8,128)(2,1)}, u32[]{:S(2)}) copy-start(bf16[768,512]{1,0:T(8,128)(2,1)} %param.13) | copy-start | bytes 2359300
  3.4 30.6 %copy-start.9 = (f32[1,2,512]{2,1,0:T(2,128)S(1)}, f32[1,2,512]{2,1,0:T(2,128)}, u32[]{:S(2)}) copy-start(f32[1,2,512]{2,1,0:T(2,128)} %param.23) | copy-start | bytes 12292
  3.4 39.5 %collective-permute-start = (bf16[4,128,512]{2,1,0:T(8,128)(2,1)}, bf16[4,128,512]{2,1,0:T(8,128)(2,1)}, u32[]{:S(2)}, u32[]{:S(2)}) collective-permute-start(bf16[4,128,512]{2,1,0:T(8,128)(2,1)} %get-tuple-element.13), channel_id=1, source_target_pairs={{0,4},{4,8},{8,12},{12,16},{16,20},{20,24},{24,28},{28,32},{32,36}... | collective-permute-start | bytes 1572872 | tf_op jit(solution)/shard_map/ppermute | solution.py:12
  5.5 42.6 %collective-permute-start.1 = (bf16[4,128,512]{2,1,0:T(8,128)(2,1)}, bf16[4,128,512]{2,1,0:T(8,128)(2,1)}, u32[]{:S(2)}, u32[]{:S(2)}) collective-permute-start(bf16[4,128,512]{2,1,0:T(8,128)(2,1)} %get-tuple-element.13), channel_id=1, source_target_pairs={{0,8},{4,12},{8,16},{12,20},{16,24},{20,28},{24,32},{28,36},{32,40... | collective-permute-start | bytes 1572872 | tf_op jit(solution)/shard_map/ppermute | solution.py:12
  9.0 42.2 %collective-permute-start.2 = (bf16[4,128,512]{2,1,0:T(8,128)(2,1)}, bf16[4,128,512]{2,1,0:T(8,128)(2,1)}, u32[]{:S(2)}, u32[]{:S(2)}) collective-permute-start(bf16[4,128,512]{2,1,0:T(8,128)(2,1)} %get-tuple-element.13), channel_id=1, source_target_pairs={{0,12},{4,16},{8,20},{12,24},{16,28},{20,32},{24,36},{28,40},{32,4... | collective-permute-start | bytes 1572872 | tf_op jit(solution)/shard_map/ppermute | solution.py:12
  13.5 39.5 %collective-permute-start.3 = (bf16[4,128,512]{2,1,0:T(8,128)(2,1)}, bf16[4,128,512]{2,1,0:T(8,128)(2,1)}, u32[]{:S(2)}, u32[]{:S(2)}) collective-permute-start(bf16[4,128,512]{2,1,0:T(8,128)(2,1)} %get-tuple-element.13), channel_id=1, source_target_pairs={{0,508},{4,0},{8,4},{12,8},{16,12},{20,16},{24,20},{28,24},{32,28}... | collective-permute-start | bytes 1572872 | tf_op jit(solution)/shard_map/ppermute | solution.py:12
  22.7 32.3 %collective-permute-start.4 = (bf16[4,128,512]{2,1,0:T(8,128)(2,1)}, bf16[4,128,512]{2,1,0:T(8,128)(2,1)}, u32[]{:S(2)}, u32[]{:S(2)}) collective-permute-start(bf16[4,128,512]{2,1,0:T(8,128)(2,1)} %get-tuple-element.13), channel_id=1, source_target_pairs={{0,504},{4,508},{8,0},{12,4},{16,8},{20,12},{24,16},{28,20},{32,24... | collective-permute-start | bytes 1572872 | tf_op jit(solution)/shard_map/ppermute | solution.py:12
  42.9 21.7 %collective-permute-start.5 = (bf16[4,128,512]{2,1,0:T(8,128)(2,1)}, bf16[4,128,512]{2,1,0:T(8,128)(2,1)S(1)}, u32[]{:S(2)}, u32[]{:S(2)}) collective-permute-start(bf16[4,128,512]{2,1,0:T(8,128)(2,1)} %get-tuple-element.13), channel_id=1, source_target_pairs={{0,500},{4,504},{8,508},{12,0},{16,4},{20,8},{24,12},{28,16},{32,2... | collective-permute-start | bytes 1572872 | tf_op jit(solution)/shard_map/ppermute | solution.py:12
  72.3 8.5 %copy-start.4 = (f32[768,512]{1,0:T(8,128)S(1)}, f32[768,512]{1,0:T(8,128)}, u32[]{:S(2)}) copy-start(f32[768,512]{1,0:T(8,128)} %fusion.23) | copy-start | bytes 4718596
  88.9 1.4 %copy-start.3 = (f32[768,512]{0,1:T(8,128)S(1)}, f32[768,512]{0,1:T(8,128)}, u32[]{:S(2)}) copy-start(f32[768,512]{0,1:T(8,128)} %copy.34) | copy-start | bytes 4718596
  90.3 2.7 %copy-start.5 = (f32[4,128,512]{2,1,0:T(8,128)S(1)}, f32[4,128,512]{2,1,0:T(8,128)}, u32[]{:S(2)}) copy-start(f32[4,128,512]{2,1,0:T(8,128)} %fusion.20) | copy-start | bytes 3145732
where the time goes:
time: 130 us
  local copies, waits for them, and re-layouts  36.8 us (28%)
  blocking collectives  28.9 us (22%)
  starting transfers between devices  26.6 us (20%)
  matrix products  22.8 us (18%)
  waiting for transfers between devices  9.11 us (7%)
  other arithmetic  3.86 us (3%)
  between operations  1.62 us (1%)
    all_to_all x1, blocking collectives, copy_for_each(): return lax.all_to_all(copies, axis, split_axis=0, concat_axis=0, tiled=True)  28.9 us
    ppermute x6, starting transfers between devices, from_behind(): return lax.ppermute(value, axis, pairs)  26.6 us
    unnamed x29, local copies, waits for them, and re-layouts  10 us
    ppermute x6, waiting for transfers between devices, from_behind(): return lax.ppermute(value, axis, pairs)  9.11 us
    gather x1, local copies, waits for them, and re-layouts, local(): senders = jnp.take(row_table, row_index, axis=1)  8.45 us
    dot_general x1, matrix products, edge_update(): jnp.einsum('mel,lk->mek', activated, weight_out, preferred_element_type=j...  8.13 us
    concatenate x2, local copies, waits for them, and re-layouts, local(): row_table = jnp.concatenate(pieces, axis=1)  7.63 us
    gather x1, local copies, waits for them, and re-layouts, local(): dest_proj = jnp.take(receiver_proj, dst_node, axis=1)  6.04 us
  transfers between devices with their start and end apart: 6, of which 2 were waited for; matrix products, arithmetic and copies ran while one was open for 19% of the time, Pallas kernels for 0%

commit v1 on v0

v1 whole, which is shorter than its diff:
```python
import jax
import jax.numpy as jnp
from jax import lax
from jax.experimental import pallas as pl
from jax.experimental.pallas import tpu as pltpu
from jax.sharding import PartitionSpec as P

RADIUS = 3
CAP = 32
EPS = 1e-05
MESH = pl.DeviceIdType.MESH
F32 = jnp.float32
BF16 = jnp.bfloat16
OFFSETS = tuple(range(1, RADIUS + 1)) + tuple(-r for r in range(1, RADIUS + 1))


def dot_nn(a, b):
    return lax.dot_general(a, b, (((1,), (0,)), ((), ())), preferred_element_type=F32)


def dot_nt(a, b):
    return lax.dot_general(a, b, (((1,), (1,)), ((), ())), preferred_element_type=F32)


def normed(values, gain):
    mean = jnp.mean(values, axis=-1, keepdims=True)
    cen = values - mean
    var = jnp.mean(cen * cen, axis=-1, keepdims=True)
    return cen * lax.rsqrt(var + EPS) * gain


def make_kernel(groups, peers, members, blk, slots, width, nbrs, layouts):
    near = len(OFFSETS)
    halo = near * CAP
    rows = blk // peers
    chunk = 256
    halo_at = 2 * blk

    def kernel(
        node_hbm, edge_hbm, nbr_hbm, src_hbm, dst_hbm, cnt_hbm,
        win_hbm, wout_hbm, nin_hbm, nout_hbm, bias_hbm, gain_hbm,
        mean_ref, spread_ref,
        node_v, edge_v, win_v, wout_v, nin_v, nout_v, bias_v, gain_v,
        src_v, dst_v, nbr_s, cnt_s,
        ask_out, ask_in, table, outbox, hot, eproj, nproj, dhot, fin, pool, result,
        in_sems, ask_ssem, ask_rsem, row_ssem, row_rsem, fin_ssem, fin_rsem, res_ssem, res_rsem,
    ):
        me = lax.axis_index("graph")
        col = lax.axis_index("member")
        near_ids = [lax.rem(me + off + groups, groups) for off in OFFSETS]
        back_ids = [lax.rem(me - off + groups, groups) for off in OFFSETS]
        peer_ids = [lax.rem(col + d, peers) for d in range(1, peers)]

        barrier = pltpu.get_barrier_semaphore()
        for g in near_ids:
            pl.semaphore_signal(barrier, inc=1, device_id={"graph": g, "member": col}, device_id_type=MESH)
        for x in peer_ids:
            pl.semaphore_signal(barrier, inc=1, device_id={"graph": me, "member": x}, device_id_type=MESH)

        loads = [
            (src_hbm, src_v), (nbr_hbm, nbr_s), (cnt_hbm, cnt_s), (dst_hbm, dst_v),
            (win_hbm.at[0, 1], win_v.at[1]), (node_hbm, node_v), (bias_hbm.at[0], bias_v), (gain_hbm.at[0], gain_v),
            (win_hbm.at[0, 2], win_v.at[2]), (nin_hbm.at[0, 0], nin_v.at[0]),
            (win_hbm.at[0, 0], win_v.at[0]), (edge_hbm, edge_v), (wout_hbm.at[0], wout_v),
            (nin_hbm.at[0, 1], nin_v.at[1]), (nout_hbm.at[0], nout_v),
        ]
        copies = [pltpu.make_async_copy(s, d, in_sems.at[i]) for i, (s, d) in enumerate(loads)]
        for c in copies:
            c.start()

        for c in copies[:4]:
            c.wait()
        lane_e = lax.broadcasted_iota(jnp.int32, (1, slots), 1)
        src = src_v[...]
        slot = src // blk
        node = src - slot * blk
        live = lane_e < cnt_s[0]
        place = jnp.full((1, slots), near, jnp.int32)
        for s in range(nbrs):
            dist = lax.rem(nbr_s[0, s] - me + groups, groups)
            p = jnp.where(dist <= RADIUS, dist - 1, RADIUS - 1 + groups - dist)
            place = jnp.where(slot == s, p, place)
        sub8 = lax.broadcasted_iota(jnp.int32, (8, slots), 0)
        subn = lax.broadcasted_iota(jnp.int32, (blk, slots), 0)
        near_hot = jnp.where((sub8 == place) & live, 1.0, 0.0).astype(BF16)
        node_hot = jnp.where(subn == node, 1.0, 0.0).astype(BF16)
        used = jnp.where(dot_nt(near_hot, node_hot) > 0.5, 1.0, 0.0)
        sq_r = lax.broadcasted_iota(jnp.int32, (blk, blk), 0)
        sq_c = lax.broadcasted_iota(jnp.int32, (blk, blk), 1)
        before = jnp.where(sq_r < sq_c, 1.0, 0.0).astype(BF16)
        rank = jnp.where(used > 0.5, dot_nn(used.astype(BF16), before), 1000.0)
        for p in range(near):
            ask_out[p] = jnp.broadcast_to(rank[p : p + 1, :], (8, blk))
        capf = lax.broadcasted_iota(jnp.int32, (CAP, blk), 0).astype(F32)
        mine = jnp.concatenate(
            [jnp.where(capf == rank[p : p + 1, :], 1.0, 0.0) for p in range(near)], axis=0
        ).astype(BF16)

        pl.semaphore_wait(barrier, near + peers - 1)

        def ask(p):
            return pltpu.make_async_remote_copy(
                src_ref=ask_out.at[p], dst_ref=ask_in.at[p], send_sem=ask_ssem.at[p], recv_sem=ask_rsem.at[p],
                device_id={"graph": near_ids[p], "member": col}, device_id_type=MESH)

        for p in range(near):
            ask(p).start()

        for c in copies[4:8]:
            c.wait()

        def project(m, carry):
            part = dot_nn(node_v[m], win_v[1])
            table[m, 0:blk, :] = (0.5 * part).astype(BF16)
            return carry

        lax.fori_loop(0, members, project, 0)

        eye = jnp.where(sq_r == sq_c, 1.0, 0.0).astype(BF16)
        lane_n = sq_c.astype(F32)
        near_of = (lax.broadcasted_iota(jnp.int32, (blk, 2 * blk), 1) // CAP).astype(F32)
        dst = dst_v[...]
        for j in range(slots // blk):
            part = slice(j * blk, (j + 1) * blk)

            def column(row, n):
                return dot_nt(eye, jnp.broadcast_to(row[:, part].astype(F32), (n, blk)).astype(BF16))

            node_c = column(node, blk)
            dst_c = column(dst, blk)
            place_c = column(place, 2 * blk)
            one = jnp.where(node_c == lane_n, 1.0, 0.0)
            hot[part, 0:blk] = jnp.where(place_c[:, 0:blk] == float(near), one, 0.0).astype(BF16)
            hot[part, blk : 2 * blk] = jnp.where(dst_c == lane_n, 1.0, 0.0).astype(BF16)
            pick = dot_nt(one.astype(BF16), mine)
            pick = jnp.concatenate([pick, jnp.zeros((blk, 2 * blk - halo), F32)], axis=1)
            hot[part, 2 * blk : 4 * blk] = jnp.where(place_c == near_of, pick, 0.0).astype(BF16)
        dhot[...] = jnp.where((subn == dst) & live, 1.0, 0.0).astype(BF16)

        for p in range(near):
            ask(p).wait_recv()
        theirs = jnp.concatenate(
            [jnp.where(capf == ask_in[p, 0:1, :], 1.0, 0.0) for p in range(near)], axis=0
        ).astype(BF16)

        def rows_to(m, p):
            return pltpu.make_async_remote_copy(
                src_ref=outbox.at[m, pl.ds(p * CAP, CAP), :],
                dst_ref=table.at[m, pl.ds(halo_at + p * CAP, CAP), :],
                send_sem=row_ssem.at[m, p], recv_sem=row_rsem.at[m, p],
                device_id={"graph": back_ids[p], "member": col}, device_id_type=MESH)

        def select(m, carry):
            outbox[m] = dot_nn(theirs, table[m, 0:blk, :]).astype(BF16)
            for p in range(near):
                rows_to(m, p).start()
            return carry

        lax.fori_loop(0, members, select, 0)

        for c in copies[8:]:
            c.wait()

        def project_more(m, carry):
            x = node_v[m]
            table[m, blk : 2 * blk, :] = (0.5 * dot_nn(x, win_v[2])).astype(BF16)
            table[m, halo_at + halo :, :] = jnp.zeros((4 * blk - halo_at - halo, width), BF16)
            nproj[m] = 0.5 * (dot_nn(x, nin_v[0]) + bias_v[2:3, :])
            return carry

        lax.fori_loop(0, members, project_more, 0)

        def project_edges(j, carry):
            part = pl.ds(pl.multiple_of(j * chunk, chunk), chunk)
            eproj[part, :] = 0.5 * (dot_nn(edge_v[part, :], win_v[0]) + bias_v[0:1, :])
            return carry

        lax.fori_loop(0, slots // chunk, project_edges, 0)

        def fin_to(m, d):
            return pltpu.make_async_remote_copy(
                src_ref=fin.at[m, pl.ds(pl.multiple_of(peer_ids[d] * rows, rows), rows), :],
                dst_ref=pool.at[col * members + m],
                send_sem=fin_ssem.at[m, d], recv_sem=fin_rsem.at[m, d],
                device_id={"graph": me, "member": peer_ids[d]}, device_id_type=MESH)

        def one_member(m, carry):
            for p in range(near):
                rows_to(m, p).wait_recv()
            total = jnp.zeros((blk, width), F32)
            for j in range(slots // chunk):
                part = slice(j * chunk, (j + 1) * chunk)
                half = dot_nn(hot[part, :], table[m]) + eproj[part, :]
                act = (half + half * jnp.tanh(half)).astype(BF16)
                mixed = dot_nn(act, wout_v[...]) + bias_v[1:2, :]
                new = (edge_v[part, :].astype(F32) + normed(mixed, gain_v[0:1, :])).astype(BF16)
                total = total + dot_nn(dhot[:, part], new)
            nhalf = 0.5 * dot_nn(total.astype(BF16), nin_v[1]) + nproj[m]
            nact = (nhalf + nhalf * jnp.tanh(nhalf)).astype(BF16)
            nmixed = dot_nn(nact, nout_v[...]) + bias_v[3:4, :]
            fin[m] = (node_v[m].astype(F32) + normed(nmixed, gain_v[1:2, :])).astype(BF16)
            pool[col * members + m] = fin[m, pl.ds(pl.multiple_of(col * rows, rows), rows), :]
            for d in range(peers - 1):
                fin_to(m, d).start()
            return carry

        lax.fori_loop(0, members, one_member, 0)

        def await_fin(m, carry):
            for d in range(peers - 1):
                fin_to(m, d).wait_recv()
            return carry

        lax.fori_loop(0, members, await_fin, 0)
        count = members * peers
        total = jnp.zeros((rows, width), F32)
        for i in range(count):
            total = total + pool[i].astype(F32)
        centre = total / count
        square = jnp.zeros((rows, width), F32)
        for i in range(count):
            dev = pool[i].astype(F32) - centre
            square = square + dev * dev
        result[col, 0] = centre.astype(BF16)
        result[col, 1] = jnp.sqrt(square / count).astype(BF16)

        def res_to(d):
            return pltpu.make_async_remote_copy(
                src_ref=result.at[col], dst_ref=result.at[col],
                send_sem=res_ssem.at[d], recv_sem=res_rsem.at[d],
                device_id={"graph": me, "member": peer_ids[d]}, device_id_type=MESH)

        for d in range(peers - 1):
            res_to(d).start()
        for d in range(peers - 1):
            res_to(d).wait_recv()
        for x in range(peers):
            mean_ref[x * rows : (x + 1) * rows, :] = result[x, 0]
            spread_ref[x * rows : (x + 1) * rows, :] = result[x, 1]

        for p in range(near):
            ask(p).wait_send()

        def drain(m, carry):
            for p in range(near):
                rows_to(m, p).wait_send()
            for d in range(peers - 1):
                fin_to(m, d).wait_send()
            return carry

        lax.fori_loop(0, members, drain, 0)
        for d in range(peers - 1):
            res_to(d).wait_send()

    return kernel


def local(node_latents, edge_latents, neighbours, edge_source, edge_dest, edge_count,
          edge_in, edge_out, node_in, node_out, biases, gains):
    members, blk, width = node_latents.shape
    slots = edge_source.shape[1]
    nbrs = neighbours.shape[1]
    groups = lax.axis_size("graph")
    peers = lax.axis_size("member")
    near = len(OFFSETS)
    halo = near * CAP
    rows = blk // peers
    vm = pltpu.VMEM
    dma = pltpu.SemaphoreType.DMA
    scratch = [
        vm((members, blk, width), BF16), vm((slots, width), BF16), vm((3, width, width), BF16),
        vm((width, width), BF16), vm((2, width, width), BF16), vm((width, width), BF16),
        vm((4, width), F32), vm((2, width), F32),
        vm((1, slots), jnp.int32), vm((1, slots), jnp.int32),
        pltpu.SMEM((1, nbrs), jnp.int32), pltpu.SMEM((1,), jnp.int32),
        vm((near, 8, blk), F32), vm((near, 8, blk), F32),
        vm((members, 4 * blk, width), BF16), vm((members, halo, width), BF16),
        vm((slots, 4 * blk), BF16), vm((slots, width), F32), vm((members, blk, width), F32),
        vm((blk, slots), BF16), vm((members, blk, width), BF16), vm((members * peers, rows, width), BF16),
        vm((peers, 2, rows, width), BF16),
        dma((15,)), dma((near,)), dma((near,)), dma((members, near)), dma((members, near)),
        dma((members, peers - 1)), dma((members, peers - 1)), dma((peers - 1,)), dma((peers - 1,)),
    ]
    out = jax.ShapeDtypeStruct((blk, width), BF16)
    return pl.pallas_call(
        make_kernel(groups, peers, members, blk, slots, width, nbrs, None),
        out_shape=(out, out),
        in_specs=[pl.BlockSpec(memory_space=pltpu.HBM)] * 12,
        out_specs=(pl.BlockSpec(memory_space=pltpu.VMEM),) * 2,
        scratch_shapes=scratch,
        compiler_params=pltpu.CompilerParams(
            collective_id=0, has_side_effects=True, vmem_limit_bytes=48 * 1024 * 1024
        ),
    )(node_latents, edge_latents, neighbours, edge_source, edge_dest, edge_count,
      edge_in, edge_out, node_in, node_out, biases, gains)


def solution(mesh):
    return jax.shard_map(
        local,
        mesh=mesh,
        in_specs=(
            P("member", "graph", None), P("graph", None), P("graph", None), P("graph", None),
            P("graph", None), P("graph"), P(), P(), P(), P(), P(), P(),
        ),
        out_specs=(P("graph", None), P("graph", None)),
        check_vma=False,
    )
```

time: 130 us -> 58.1 us (0.45)
  the two profiles are of different devices: /device:TPU:2 before, /device:TPU:4 now
where the time goes in v1:
time: 58.1 us; the launch traced here: 57.6 us
  Pallas kernels  44.7 us (77%)
  local copies, waits for them, and re-layouts  11.6 us (20%)
  between operations  1.31 us (2%)
    pallas_call x1, Pallas kernels, local(): pl.pallas_call(make_kernel(groups, peers, members, blk, slots, width, nbr...  44.7 us
    unnamed x24, local copies, waits for them, and re-layouts  11.6 us

profile of v1, /device:TPU:4, one launch (start us, length us, event | category | flops | bytes accessed | tf_op | source)
XLA Modules:
  0.0 57.6 jit_solution(16730262349205417721)
XLA Ops:
  1.3 0.0 copy-start
  1.3 1.4 %copy-done = bf16[1,3,512,512]{3,2,1,0:T(8,128)(2,1)S(1)} copy-done((bf16[1,3,512,512]{3,2,1,0:T(8,128)(2,1)S(1)}, bf16[1,3,512,512]{3,2,1,0:T(8,128)(2,1)}, u32[]{:S(2)}) %copy-start) | copy-done | bytes 1572888
  2.7 0.0 copy-start.1
  2.7 1.2 %copy-done.1 = bf16[1,2,512,512]{3,2,1,0:T(8,128)(2,1)S(1)} copy-done((bf16[1,2,512,512]{3,2,1,0:T(8,128)(2,1)S(1)}, bf16[1,2,512,512]{3,2,1,0:T(8,128)(2,1)}, u32[]{:S(2)}) %copy-start.1) | copy-done | bytes 1048600
  3.9 0.0 copy-start.2
  3.9 1.1 %copy-done.2 = bf16[768,512]{1,0:T(8,128)(2,1)S(1)} copy-done((bf16[768,512]{1,0:T(8,128)(2,1)S(1)}, bf16[768,512]{1,0:T(8,128)(2,1)}, u32[]{:S(2)}) %copy-start.2) | copy-done | bytes 786456
  5.0 0.0 copy-start.3
  5.0 1.0 %copy-done.3 = bf16[4,128,512]{2,1,0:T(8,128)(2,1)S(1)} copy-done((bf16[4,128,512]{2,1,0:T(8,128)(2,1)S(1)}, bf16[4,128,512]{2,1,0:T(8,128)(2,1)}, u32[]{:S(2)}) %copy-start.3) | copy-done | bytes 524312
  6.1 0.0 copy-start.4
  6.1 1.0 %copy-done.4 = bf16[1,512,512]{2,1,0:T(8,128)(2,1)S(1)} copy-done((bf16[1,512,512]{2,1,0:T(8,128)(2,1)S(1)}, bf16[1,512,512]{2,1,0:T(8,128)(2,1)}, u32[]{:S(2)}) %copy-start.4) | copy-done | bytes 524312
  7.1 0.0 copy-start.5
  7.1 1.0 %copy-done.5 = bf16[1,512,512]{2,1,0:T(8,128)(2,1)S(1)} copy-done((bf16[1,512,512]{2,1,0:T(8,128)(2,1)S(1)}, bf16[1,512,512]{2,1,0:T(8,128)(2,1)}, u32[]{:S(2)}) %copy-start.5) | copy-done | bytes 524312
  8.2 0.0 copy-start.6
  8.2 0.7 %copy-done.6 = f32[1,4,512]{2,1,0:T(4,128)S(1)} copy-done((f32[1,4,512]{2,1,0:T(4,128)S(1)}, f32[1,4,512]{2,1,0:T(4,128)}, u32[]{:S(2)}) %copy-start.6) | copy-done | bytes 8216
  8.9 0.0 copy-start.7
  8.9 0.7 %copy-done.7 = f32[1,2,512]{2,1,0:T(2,128)S(1)} copy-done((f32[1,2,512]{2,1,0:T(2,128)S(1)}, f32[1,2,512]{2,1,0:T(2,128)}, u32[]{:S(2)}) %copy-start.7) | copy-done | bytes 4120
  9.6 0.0 copy-start.8
  9.6 0.7 %copy-done.8 = s32[1,768]{1,0:T(1,128)S(1)} copy-done((s32[1,768]{1,0:T(1,128)S(1)}, s32[1,768]{1,0:T(1,128)}, u32[]{:S(2)}) %copy-start.8) | copy-done | bytes 3096
  10.2 0.0 copy-start.9
  10.2 0.7 %copy-done.9 = s32[1,768]{1,0:T(1,128)S(1)} copy-done((s32[1,768]{1,0:T(1,128)S(1)}, s32[1,768]{1,0:T(1,128)}, u32[]{:S(2)}) %copy-start.9) | copy-done | bytes 3096
  10.9 0.0 copy-start.10
  10.9 0.7 %copy-done.10 = s32[1,4]{1,0:T(1,128)S(1)} copy-done((s32[1,4]{1,0:T(1,128)S(1)}, s32[1,4]{1,0:T(1,128)}, u32[]{:S(2)}) %copy-start.10) | copy-done | bytes 40
  11.6 44.7 %shard_map.131 = (bf16[128,512]{1,0:T(8,128)(2,1)S(1)}, bf16[128,512]{1,0:T(8,128)(2,1)S(1)}) custom-call(bf16[4,128,512]{2,1,0:T(8,128)(2,1)S(1)} %copy-done.3, bf16[768,512]{1,0:T(8,128)(2,1)S(1)} %copy-done.2, s32[1,4]{1,0:T(1,128)S(1)} %copy-done.10, s32[1,768]{1,0:T(1,128)S(1)} %copy-done.8, s32[1,768]{1,0:T(1,128)S(1)} %copy-done.9, ...), custom_call_target="tpu_custom_call" | custom-call | tf_op jit(solution)/shard_map/pallas_call | solution.py:285
  56.3 0.7 %copy.17 = bf16[128,512]{1,0:T(8,128)(2,1)} copy(bf16[128,512]{1,0:T(8,128)(2,1)S(1)} %get-tuple-element.4) | data formatting | bytes 262144
  56.9 0.7 %copy.18 = bf16[128,512]{1,0:T(8,128)(2,1)} copy(bf16[128,512]{1,0:T(8,128)(2,1)S(1)} %get-tuple-element.5) | data formatting | bytes 262144
Async XLA Ops:
  1.3 1.4 %copy-start = (bf16[1,3,512,512]{3,2,1,0:T(8,128)(2,1)S(1)}, bf16[1,3,512,512]{3,2,1,0:T(8,128)(2,1)}, u32[]{:S(2)}) copy-start(bf16[1,3,512,512]{3,2,1,0:T(8,128)(2,1)} %win_hbm.1) | copy-start | bytes 4718596
  2.7 1.2 %copy-start.1 = (bf16[1,2,512,512]{3,2,1,0:T(8,128)(2,1)S(1)}, bf16[1,2,512,512]{3,2,1,0:T(8,128)(2,1)}, u32[]{:S(2)}) copy-start(bf16[1,2,512,512]{3,2,1,0:T(8,128)(2,1)} %nin_hbm.1) | copy-start | bytes 3145732
  3.9 1.1 %copy-start.2 = (bf16[768,512]{1,0:T(8,128)(2,1)S(1)}, bf16[768,512]{1,0:T(8,128)(2,1)}, u32[]{:S(2)}) copy-start(bf16[768,512]{1,0:T(8,128)(2,1)} %edge_hbm.1) | copy-start | bytes 2359300
  5.0 1.0 %copy-start.3 = (bf16[4,128,512]{2,1,0:T(8,128)(2,1)S(1)}, bf16[4,128,512]{2,1,0:T(8,128)(2,1)}, u32[]{:S(2)}) copy-start(bf16[4,128,512]{2,1,0:T(8,128)(2,1)} %node_hbm.1) | copy-start | bytes 1572868
  6.1 1.0 %copy-start.4 = (bf16[1,512,512]{2,1,0:T(8,128)(2,1)S(1)}, bf16[1,512,512]{2,1,0:T(8,128)(2,1)}, u32[]{:S(2)}) copy-start(bf16[1,512,512]{2,1,0:T(8,128)(2,1)} %wout_hbm.1) | copy-start | bytes 1572868
  7.1 1.0 %copy-start.5 = (bf16[1,512,512]{2,1,0:T(8,128)(2,1)S(1)}, bf16[1,512,512]{2,1,0:T(8,128)(2,1)}, u32[]{:S(2)}) copy-start(bf16[1,512,512]{2,1,0:T(8,128)(2,1)} %nout_hbm.1) | copy-start | bytes 1572868
  8.2 0.7 %copy-start.6 = (f32[1,4,512]{2,1,0:T(4,128)S(1)}, f32[1,4,512]{2,1,0:T(4,128)}, u32[]{:S(2)}) copy-start(f32[1,4,512]{2,1,0:T(4,128)} %bias_hbm.1) | copy-start | bytes 24580
  8.9 0.7 %copy-start.7 = (f32[1,2,512]{2,1,0:T(2,128)S(1)}, f32[1,2,512]{2,1,0:T(2,128)}, u32[]{:S(2)}) copy-start(f32[1,2,512]{2,1,0:T(2,128)} %gain_hbm.1) | copy-start | bytes 12292
  9.6 0.7 %copy-start.8 = (s32[1,768]{1,0:T(1,128)S(1)}, s32[1,768]{1,0:T(1,128)}, u32[]{:S(2)}) copy-start(s32[1,768]{1,0:T(1,128)} %src_hbm.1) | copy-start | bytes 9220
  10.2 0.7 %copy-start.9 = (s32[1,768]{1,0:T(1,128)S(1)}, s32[1,768]{1,0:T(1,128)}, u32[]{:S(2)}) copy-start(s32[1,768]{1,0:T(1,128)} %dst_hbm.1) | copy-start | bytes 9220
  10.9 0.7 %copy-start.10 = (s32[1,4]{1,0:T(1,128)S(1)}, s32[1,4]{1,0:T(1,128)}, u32[]{:S(2)}) copy-start(s32[1,4]{1,0:T(1,128)} %nbr_hbm.1) | copy-start | bytes 52

commit v2 on v1

--- a/solution.py
+++ b/solution.py
@@ -29,20 +29,19 @@
     return cen * lax.rsqrt(var + EPS) * gain
 
 
-def make_kernel(groups, peers, members, blk, slots, width, nbrs, layouts):
+def make_kernel(groups, peers, members, blk, slots, width, nbrs):
     near = len(OFFSETS)
     halo = near * CAP
     rows = blk // peers
     chunk = 256
-    halo_at = 2 * blk
 
     def kernel(
-        node_hbm, edge_hbm, nbr_hbm, src_hbm, dst_hbm, cnt_hbm,
+        node_hbm, edge_hbm, nbr_hbm, src_hbm, dst_hbm, cnt_ref,
         win_hbm, wout_hbm, nin_hbm, nout_hbm, bias_hbm, gain_hbm,
         mean_ref, spread_ref,
         node_v, edge_v, win_v, wout_v, nin_v, nout_v, bias_v, gain_v,
-        src_v, dst_v, nbr_s, cnt_s,
-        ask_out, ask_in, table, outbox, hot, eproj, nproj, dhot, fin, pool, result,
+        src_v, dst_v, nbr_s,
+        ask_out, ask_in, own, halo_in, outbox, hot, far_hot, eproj, pre, nproj, dhot, fin, pool, result,
         in_sems, ask_ssem, ask_rsem, row_ssem, row_rsem, fin_ssem, fin_rsem, res_ssem, res_rsem,
     ):
         me = lax.axis_index("graph")
@@ -58,23 +57,23 @@
             pl.semaphore_signal(barrier, inc=1, device_id={"graph": me, "member": x}, device_id_type=MESH)
 
         loads = [
-            (src_hbm, src_v), (nbr_hbm, nbr_s), (cnt_hbm, cnt_s), (dst_hbm, dst_v),
+            (src_hbm, src_v), (nbr_hbm, nbr_s), (dst_hbm, dst_v),
             (win_hbm.at[0, 1], win_v.at[1]), (node_hbm, node_v), (bias_hbm.at[0], bias_v), (gain_hbm.at[0], gain_v),
-            (win_hbm.at[0, 2], win_v.at[2]), (nin_hbm.at[0, 0], nin_v.at[0]),
-            (win_hbm.at[0, 0], win_v.at[0]), (edge_hbm, edge_v), (wout_hbm.at[0], wout_v),
+            (win_hbm.at[0, 2], win_v.at[2]), (win_hbm.at[0, 0], win_v.at[0]), (edge_hbm, edge_v),
+            (nin_hbm.at[0, 0], nin_v.at[0]), (wout_hbm.at[0], wout_v),
             (nin_hbm.at[0, 1], nin_v.at[1]), (nout_hbm.at[0], nout_v),
         ]
         copies = [pltpu.make_async_copy(s, d, in_sems.at[i]) for i, (s, d) in enumerate(loads)]
         for c in copies:
             c.start()
 
-        for c in copies[:4]:
+        for c in copies[:3]:
             c.wait()
         lane_e = lax.broadcasted_iota(jnp.int32, (1, slots), 1)
         src = src_v[...]
         slot = src // blk
         node = src - slot * blk
-        live = lane_e < cnt_s[0]
+        live = lane_e < cnt_ref[0]
         place = jnp.full((1, slots), near, jnp.int32)
         for s in range(nbrs):
             dist = lax.rem(nbr_s[0, s] - me + groups, groups)
@@ -96,6 +95,16 @@
             [jnp.where(capf == rank[p : p + 1, :], 1.0, 0.0) for p in range(near)], axis=0
         ).astype(BF16)
 
+        for c in copies[3:7]:
+            c.wait()
+
+        def project(m, carry):
+            part = dot_nn(node_v[m], win_v[1])
+            own[m, 0:blk, :] = (0.5 * part).astype(BF16)
+            return carry
+
+        lax.fori_loop(0, members, project, 0)
+
         pl.semaphore_wait(barrier, near + peers - 1)
 
         def ask(p):
@@ -105,16 +114,6 @@
 
         for p in range(near):
             ask(p).start()
-
-        for c in copies[4:8]:
-            c.wait()
-
-        def project(m, carry):
-            part = dot_nn(node_v[m], win_v[1])
-            table[m, 0:blk, :] = (0.5 * part).astype(BF16)
-            return carry
-
-        lax.fori_loop(0, members, project, 0)
 
         eye = jnp.where(sq_r == sq_c, 1.0, 0.0).astype(BF16)
         lane_n = sq_c.astype(F32)
@@ -134,8 +133,25 @@
             hot[part, blk : 2 * blk] = jnp.where(dst_c == lane_n, 1.0, 0.0).astype(BF16)
             pick = dot_nt(one.astype(BF16), mine)
             pick = jnp.concatenate([pick, jnp.zeros((blk, 2 * blk - halo), F32)], axis=1)
-            hot[part, 2 * blk : 4 * blk] = jnp.where(place_c == near_of, pick, 0.0).astype(BF16)
+            far_hot[part, :] = jnp.where(place_c == near_of, pick, 0.0).astype(BF16)
         dhot[...] = jnp.where((subn == dst) & live, 1.0, 0.0).astype(BF16)
+
+        for c in copies[7:10]:
+            c.wait()
+
+        def project_receivers(m, carry):
+            own[m, blk : 2 * blk, :] = (0.5 * dot_nn(node_v[m], win_v[2])).astype(BF16)
+            halo_in[m, halo:, :] = jnp.zeros((2 * blk - halo, width), BF16)
+            return carry
+
+        lax.fori_loop(0, members, project_receivers, 0)
+
+        def project_edges(j, carry):
+            part = pl.ds(pl.multiple_of(j * chunk, chunk), chunk)
+            eproj[part, :] = 0.5 * (dot_nn(edge_v[part, :], win_v[0]) + bias_v[0:1, :])
+            return carry
+
+        lax.fori_loop(0, slots // chunk, project_edges, 0)
 
         for p in range(near):
             ask(p).wait_recv()
@@ -146,36 +162,34 @@
         def rows_to(m, p):
             return pltpu.make_async_remote_copy(
                 src_ref=outbox.at[m, pl.ds(p * CAP, CAP), :],
-                dst_ref=table.at[m, pl.ds(halo_at + p * CAP, CAP), :],
+                dst_ref=halo_in.at[m, pl.ds(p * CAP, CAP), :],
                 send_sem=row_ssem.at[m, p], recv_sem=row_rsem.at[m, p],
                 device_id={"graph": back_ids[p], "member": col}, device_id_type=MESH)
 
         def select(m, carry):
-            outbox[m] = dot_nn(theirs, table[m, 0:blk, :]).astype(BF16)
+            outbox[m] = dot_nn(theirs, own[m, 0:blk, :]).astype(BF16)
             for p in range(near):
                 rows_to(m, p).start()
             return carry
 
         lax.fori_loop(0, members, select, 0)
 
-        for c in copies[8:]:
+        for c in copies[10:]:
             c.wait()
 
-        def project_more(m, carry):
-            x = node_v[m]
-            table[m, blk : 2 * blk, :] = (0.5 * dot_nn(x, win_v[2])).astype(BF16)
-            table[m, halo_at + halo :, :] = jnp.zeros((4 * blk - halo_at - halo, width), BF16)
-            nproj[m] = 0.5 * (dot_nn(x, nin_v[0]) + bias_v[2:3, :])
-            return carry
-
-        lax.fori_loop(0, members, project_more, 0)
-
-        def project_edges(j, carry):
-            part = pl.ds(pl.multiple_of(j * chunk, chunk), chunk)
-            eproj[part, :] = 0.5 * (dot_nn(edge_v[part, :], win_v[0]) + bias_v[0:1, :])
-            return carry
-
-        lax.fori_loop(0, slots // chunk, project_edges, 0)
+        def project_nodes(m, carry):
+            nproj[m] = 0.5 * (dot_nn(node_v[m], nin_v[0]) + bias_v[2:3, :])
+            return carry
+
+        lax.fori_loop(0, members, project_nodes, 0)
+
+        def precompute(m, carry):
+            for j in range(slots // chunk):
+                part = slice(j * chunk, (j + 1) * chunk)
+                pre[m, part, :] = eproj[part, :] + dot_nn(hot[part, :], own[m])
+            return carry
+
+        lax.fori_loop(0, members, precompute, 0)
 
         def fin_to(m, d):
             return pltpu.make_async_remote_copy(
@@ -187,14 +201,11 @@
         def one_member(m, carry):
             for p in range(near):
                 rows_to(m, p).wait_recv()
-            total = jnp.zeros((blk, width), F32)
-            for j in range(slots // chunk):
-                part = slice(j * chunk, (j + 1) * chunk)
-                half = dot_nn(hot[part, :], table[m]) + eproj[part, :]
-                act = (half + half * jnp.tanh(half)).astype(BF16)
-                mixed = dot_nn(act, wout_v[...]) + bias_v[1:2, :]
-                new = (edge_v[part, :].astype(F32) + normed(mixed, gain_v[0:1, :])).astype(BF16)
-                total = total + dot_nn(dhot[:, part], new)
+            half = pre[m] + dot_nn(far_hot[...], halo_in[m])
+            act = (half + half * jnp.tanh(half)).astype(BF16)
+            mixed = dot_nn(act, wout_v[...]) + bias_v[1:2, :]
+            new = (edge_v[...].astype(F32) + normed(mixed, gain_v[0:1, :])).astype(BF16)
+            total = dot_nn(dhot[...], new)
             nhalf = 0.5 * dot_nn(total.astype(BF16), nin_v[1]) + nproj[m]
             nact = (nhalf + nhalf * jnp.tanh(nhalf)).astype(BF16)
             nmixed = dot_nn(nact, nout_v[...]) + bias_v[3:4, :]
@@ -272,27 +283,31 @@
         vm((width, width), BF16), vm((2, width, width), BF16), vm((width, width), BF16),
         vm((4, width), F32), vm((2, width), F32),
         vm((1, slots), jnp.int32), vm((1, slots), jnp.int32),
-        pltpu.SMEM((1, nbrs), jnp.int32), pltpu.SMEM((1,), jnp.int32),
+        pltpu.SMEM((1, nbrs), jnp.int32),
         vm((near, 8, blk), F32), vm((near, 8, blk), F32),
-        vm((members, 4 * blk, width), BF16), vm((members, halo, width), BF16),
-        vm((slots, 4 * blk), BF16), vm((slots, width), F32), vm((members, blk, width), F32),
+        vm((members, 2 * blk, width), BF16), vm((members, 2 * blk, width), BF16), vm((members, halo, width), BF16),
+        vm((slots, 2 * blk), BF16), vm((slots, 2 * blk), BF16), vm((slots, width), F32), vm((members, slots, width), F32), vm((members, blk, width), F32),
         vm((blk, slots), BF16), vm((members, blk, width), BF16), vm((members * peers, rows, width), BF16),
         vm((peers, 2, rows, width), BF16),
-        dma((15,)), dma((near,)), dma((near,)), dma((members, near)), dma((members, near)),
+        dma((14,)), dma((near,)), dma((near,)), dma((members, near)), dma((members, near)),
         dma((members, peers - 1)), dma((members, peers - 1)), dma((peers - 1,)), dma((peers - 1,)),
     ]
     out = jax.ShapeDtypeStruct((blk, width), BF16)
+    args = [node_latents, edge_latents, neighbours, edge_source, edge_dest, edge_count,
+            edge_in, edge_out, node_in, node_out, biases, gains]
+    specs = [pl.BlockSpec(memory_space=pltpu.HBM)] * len(args)
+    specs[5] = pl.BlockSpec(memory_space=pltpu.SMEM)
+    args = [a if i == 5 else pltpu.with_memory_space_constraint(a, pltpu.HBM) for i, a in enumerate(args)]
     return pl.pallas_call(
-        make_kernel(groups, peers, members, blk, slots, width, nbrs, None),
+        make_kernel(groups, peers, members, blk, slots, width, nbrs),
         out_shape=(out, out),
-        in_specs=[pl.BlockSpec(memory_space=pltpu.HBM)] * 12,
+        in_specs=specs,
         out_specs=(pl.BlockSpec(memory_space=pltpu.VMEM),) * 2,
         scratch_shapes=scratch,
         compiler_params=pltpu.CompilerParams(
-            collective_id=0, has_side_effects=True, vmem_limit_bytes=48 * 1024 * 1024
+            collective_id=0, has_side_effects=True, vmem_limit_bytes=52 * 1024 * 1024
         ),
-    )(node_latents, edge_latents, neighbours, edge_source, edge_dest, edge_count,
-      edge_in, edge_out, node_in, node_out, biases, gains)
+    )(*args)
 
 
 def solution(mesh):

time: 58.1 us -> 45.5 us (0.78)
  the two profiles are of different devices: /device:TPU:4 before, /device:TPU:8 now
where the time goes in v2:
time: 45.5 us; the launch traced here: 45.3 us
  Pallas kernels  42.7 us (94%)
  local copies, waits for them, and re-layouts  1.31 us (3%)
  between operations  1.29 us (3%)
    pallas_call x1, Pallas kernels, local(): pl.pallas_call(make_kernel(groups, peers, members, blk, slots, width, nbr...  42.7 us
    unnamed x2, local copies, waits for them, and re-layouts  1.31 us

profile of v2, /device:TPU:8, one launch (start us, length us, event | category | flops | bytes accessed | tf_op | source)
XLA Modules:
  0.0 45.3 jit_solution(14708546440141156405)
XLA Ops:
  1.3 42.7 %shard_map.131 = (bf16[128,512]{1,0:T(8,128)(2,1)S(1)}, bf16[128,512]{1,0:T(8,128)(2,1)S(1)}) custom-call(bf16[4,128,512]{2,1,0:T(8,128)(2,1)} %node_hbm.1, bf16[768,512]{1,0:T(8,128)(2,1)} %edge_hbm.1, s32[1,4]{1,0:T(1,128)} %nbr_hbm.1, s32[1,768]{1,0:T(1,128)} %src_hbm.1, s32[1,768]{1,0:T(1,128)} %dst_hbm.1, s32[1]{0:T(128)S(6)} %copy.16.cnt_ref, ...), custom_call_target="tpu_custom_call" | custom-call | tf_op jit(solution)/shard_map/pallas_call | solution.py:301
  44.0 0.7 %copy.17 = bf16[128,512]{1,0:T(8,128)(2,1)} copy(bf16[128,512]{1,0:T(8,128)(2,1)S(1)} %get-tuple-element.4) | data formatting | bytes 262144
  44.7 0.7 %copy.18 = bf16[128,512]{1,0:T(8,128)(2,1)} copy(bf16[128,512]{1,0:T(8,128)(2,1)S(1)} %get-tuple-element.5) | data formatting | bytes 262144

commit v3 on v2

v3 whole, which is shorter than its diff:
```python
import jax
import jax.numpy as jnp
from jax import lax
from jax.experimental import pallas as pl
from jax.experimental.pallas import tpu as pltpu
from jax.sharding import PartitionSpec as P

RADIUS = 3
CAP = 32
EPS = 1e-05
PIECES = 2
MESH = pl.DeviceIdType.MESH
F32 = jnp.float32
BF16 = jnp.bfloat16
OFFSETS = tuple(range(1, RADIUS + 1)) + tuple(-r for r in range(1, RADIUS + 1))

FAR_FIRST = (2, 5, 1, 4, 0, 3)


def FAR_PEERS(peers):
    return sorted(range(1, peers), key=lambda d: -min(d, peers - d))


def dot_nn(a, b):
    return lax.dot_general(a, b, (((1,), (0,)), ((), ())), preferred_element_type=F32)


def dot_nt(a, b):
    return lax.dot_general(a, b, (((1,), (1,)), ((), ())), preferred_element_type=F32)


def normed(values, gain):
    mean = jnp.mean(values, axis=-1, keepdims=True)
    cen = values - mean
    var = jnp.mean(cen * cen, axis=-1, keepdims=True)
    return cen * lax.rsqrt(var + EPS) * gain


def make_kernel(groups, peers, members, blk, slots, width, nbrs):
    near = len(OFFSETS)
    halo = near * CAP
    rows = blk // peers
    piece = rows // PIECES

    def kernel(
        node_hbm, edge_hbm, nbr_hbm, src_hbm, dst_hbm, cnt_ref,
        win_hbm, wout_hbm, nin_hbm, nout_hbm, bias_hbm, gain_hbm,
        both_ref,
        node_v, edge_v, win_v, wout_v, nin_v, nout_v, bias_v, gain_v,
        src_v, dst_v, nbr_s,
        ask_out, ask_in, own, halo_in, outbox, hot, far_hot, eproj, pre, nproj, dhot, fin, pool, result,
        in_sems, ask_sems, row_ssem, row_rsem, fin_ssem, fin_rsem, res_ssem, res_rsem,
    ):
        me = lax.axis_index("graph")
        col = lax.axis_index("member")
        near_ids = [lax.rem(me + off + groups, groups) for off in OFFSETS]
        back_ids = [lax.rem(me - off + groups, groups) for off in OFFSETS]
        peer_ids = [lax.rem(col + d, peers) for d in FAR_PEERS(peers)]

        def load(i, s, d):
            return pltpu.make_async_copy(s, d, in_sems.at[i])

        loads = [
            (src_hbm, src_v), (nbr_hbm, nbr_s), (dst_hbm, dst_v),
            (win_hbm.at[0, 1], win_v.at[1]), (node_hbm, node_v), (bias_hbm.at[0], bias_v), (gain_hbm.at[0], gain_v),
            (win_hbm.at[0, 2], win_v.at[2]), (win_hbm.at[0, 0], win_v.at[0]), (edge_hbm, edge_v),
            (nin_hbm.at[0, 0], nin_v.at[0]), (wout_hbm.at[0], wout_v),
            (nin_hbm.at[0, 1], nin_v.at[1]), (nout_hbm.at[0], nout_v),
        ]
        copies = [load(i, s, d) for i, (s, d) in enumerate(loads)]
        for c in copies[:2]:
            c.start()
        barrier = pltpu.get_barrier_semaphore()
        for g in near_ids:
            pl.semaphore_signal(barrier, inc=1, device_id={"graph": g, "member": col}, device_id_type=MESH)
        for x in peer_ids:
            pl.semaphore_signal(barrier, inc=1, device_id={"graph": me, "member": x}, device_id_type=MESH)
        for c in copies[2:]:
            c.start()

        with jax.named_scope("s01_load"):
            for c in copies[:2]:
                c.wait()
        with jax.named_scope("s02_rank"):
            lane_e = lax.broadcasted_iota(jnp.int32, (1, slots), 1)
            src = src_v[...]
            slot = src // blk
            node = src - slot * blk
            live = lane_e < cnt_ref[0]
            place = jnp.full((1, slots), near, jnp.int32)
            for s in range(nbrs):
                dist = lax.rem(nbr_s[0, s] - me + groups, groups)
                p = jnp.where(dist <= RADIUS, dist - 1, RADIUS - 1 + groups - dist)
                place = jnp.where(slot == s, p, place)
            sub8 = lax.broadcasted_iota(jnp.int32, (8, slots), 0)
            subn = lax.broadcasted_iota(jnp.int32, (blk, slots), 0)
            near_hot = jnp.where((sub8 == place) & live, 1.0, 0.0).astype(BF16)
            node_hot = jnp.where(subn == node, 1.0, 0.0).astype(BF16)
            used = jnp.where(dot_nt(near_hot, node_hot) > 0.5, 1.0, 0.0)
            sq_r = lax.broadcasted_iota(jnp.int32, (blk, blk), 0)
            sq_c = lax.broadcasted_iota(jnp.int32, (blk, blk), 1)
            before = jnp.where(sq_r < sq_c, 1.0, 0.0).astype(BF16)
            rank = jnp.where(used > 0.5, dot_nn(used.astype(BF16), before), 1000.0)
            for p in range(near):
                ask_out[p] = jnp.broadcast_to(rank[p : p + 1, :], (8, blk))
            capf = lax.broadcasted_iota(jnp.int32, (CAP, blk), 0).astype(F32)
            mine = jnp.concatenate(
                [jnp.where(capf == rank[p : p + 1, :], 1.0, 0.0) for p in range(near)], axis=0
            ).astype(BF16)

        with jax.named_scope("s03_barrier"):
            pl.semaphore_wait(barrier, near + peers - 1)

        def ask(p):
            return pltpu.make_async_remote_copy(
                src_ref=ask_out.at[p], dst_ref=ask_in.at[p], send_sem=ask_sems.at[0], recv_sem=ask_sems.at[1],
                device_id={"graph": near_ids[p], "member": col}, device_id_type=MESH)

        for p in FAR_FIRST:
            ask(p).start()

        with jax.named_scope("s04_project"):
            for c in copies[2:5]:
                c.wait()
            part = (0.5 * dot_nn(node_v[...], win_v[1])).astype(BF16)
            for m in range(members):
                own[m, 0:blk, :] = part[m * blk : (m + 1) * blk, :]

        with jax.named_scope("s05_hot"):
            eye = jnp.where(sq_r == sq_c, 1.0, 0.0).astype(BF16)
            lane_n = sq_c.astype(F32)
            near_of = (lax.broadcasted_iota(jnp.int32, (blk, 2 * blk), 1) // CAP).astype(F32)
            dst = dst_v[...]
            for j in range(slots // blk):
                part = slice(j * blk, (j + 1) * blk)

                def column(row, n):
                    return dot_nt(eye, jnp.broadcast_to(row[:, part].astype(F32), (n, blk)).astype(BF16))

                node_c = column(node, blk)
                dst_c = column(dst, blk)
                place_c = column(place, 2 * blk)
                one = jnp.where(node_c == lane_n, 1.0, 0.0)
                hot[part, 0:blk] = jnp.where(place_c[:, 0:blk] == float(near), one, 0.0).astype(BF16)
                hot[part, blk : 2 * blk] = jnp.where(dst_c == lane_n, 1.0, 0.0).astype(BF16)
                pick = dot_nt(one.astype(BF16), mine)
                pick = jnp.concatenate([pick, jnp.zeros((blk, 2 * blk - halo), F32)], axis=1)
                far_hot[part, :] = jnp.where(place_c == near_of, pick, 0.0).astype(BF16)
            dhot[...] = jnp.where((subn == dst) & live, 1.0, 0.0).astype(BF16)

        with jax.named_scope("s06_askwait"):
            pltpu.make_async_copy(ask_in, ask_in, ask_sems.at[1]).wait()

        def rows_to(m, p):
            return pltpu.make_async_remote_copy(
                src_ref=outbox.at[m, pl.ds(p * CAP, CAP), :],
                dst_ref=halo_in.at[m, pl.ds(p * CAP, CAP), :],
                send_sem=row_ssem, recv_sem=row_rsem.at[m],
                device_id={"graph": back_ids[p], "member": col}, device_id_type=MESH)

        with jax.named_scope("s07_select"):
            theirs = jnp.concatenate(
                [jnp.where(capf == ask_in[p, 0:1, :], 1.0, 0.0) for p in range(near)], axis=0
            ).astype(BF16)

            def select(m, carry):
                outbox[m] = dot_nn(theirs, own[m, 0:blk, :]).astype(BF16)
                for p in FAR_FIRST:
                    rows_to(m, p).start()
                return carry

            lax.fori_loop(0, members, select, 0)

        with jax.named_scope("s08_recv"):
            for c in copies[5:8]:
                c.wait()
            part = (0.5 * dot_nn(node_v[...], win_v[2])).astype(BF16)
            for m in range(members):
                own[m, blk : 2 * blk, :] = part[m * blk : (m + 1) * blk, :]
                halo_in[m, halo:, :] = jnp.zeros((2 * blk - halo, width), BF16)
        with jax.named_scope("s09_eproj"):
            for c in copies[8:10]:
                c.wait()
            eproj[...] = 0.5 * (dot_nn(edge_v[...], win_v[0]) + bias_v[0:1, :])
        with jax.named_scope("s10_pre"):

            def precompute(m, carry):
                pre[m] = eproj[...] + dot_nn(hot[...], own[m])
                return carry

            lax.fori_loop(0, members, precompute, 0)
        with jax.named_scope("s11_nodes"):
            for c in copies[10:]:
                c.wait()
            nproj[...] = 0.5 * (dot_nn(node_v[...], nin_v[0]) + bias_v[2:3, :])

        def fin_to(m, d, h):
            at = pl.multiple_of(peer_ids[d] * rows + h * piece, piece)
            return pltpu.make_async_remote_copy(
                src_ref=fin.at[m, pl.ds(at, piece), :],
                dst_ref=pool.at[h, col * members + m],
                send_sem=fin_ssem, recv_sem=fin_rsem.at[h],
                device_id={"graph": me, "member": peer_ids[d]}, device_id_type=MESH)

        def one_member(m, carry):
            with jax.named_scope("m1_rowwait"):
                arrived = halo_in.at[m, pl.ds(0, halo), :]
                pltpu.make_async_copy(arrived, arrived, row_rsem.at[m]).wait()
            with jax.named_scope("m2_edge"):
                half = pre[m] + dot_nn(far_hot[...], halo_in[m])
                act = (half + half * jnp.tanh(half)).astype(BF16)
                mixed = dot_nn(act, wout_v[...]) + bias_v[1:2, :]
                new = (edge_v[...].astype(F32) + normed(mixed, gain_v[0:1, :])).astype(BF16)
                total = dot_nn(dhot[...], new)
            with jax.named_scope("m3_node"):
                mine_at = pl.ds(pl.multiple_of(m * blk, blk), blk)
                nhalf = 0.5 * dot_nn(total.astype(BF16), nin_v[1]) + nproj[mine_at, :]
                nact = (nhalf + nhalf * jnp.tanh(nhalf)).astype(BF16)
                nmixed = dot_nn(nact, nout_v[...]) + bias_v[3:4, :]
                fin[m] = (node_v[mine_at, :].astype(F32) + normed(nmixed, gain_v[1:2, :])).astype(BF16)
                for h in range(PIECES):
                    for d in range(peers - 1):
                        fin_to(m, d, h).start()
                for h in range(PIECES):
                    at = pl.multiple_of(col * rows + h * piece, piece)
                    pool[h, col * members + m] = fin[m, pl.ds(at, piece), :]
            return carry

        lax.fori_loop(0, members, one_member, 0)

        with jax.named_scope("t0_drain"):
            pltpu.make_async_copy(ask_out, ask_out, ask_sems.at[0]).wait()
            pltpu.make_async_copy(outbox, outbox, row_ssem).wait()

        def res_to(d, h):
            return pltpu.make_async_remote_copy(
                src_ref=result.at[h, col], dst_ref=result.at[h, col],
                send_sem=res_ssem, recv_sem=res_rsem,
                device_id={"graph": me, "member": peer_ids[d]}, device_id_type=MESH)

        count = members * peers
        for h in range(PIECES):
            others = pool.at[h, pl.ds(0, members * (peers - 1))]
            with jax.named_scope("t1_finwait"):
                pltpu.make_async_copy(others, others, fin_rsem.at[h]).wait()
            with jax.named_scope("t2_final"):
                total = jnp.zeros((piece, width), F32)
                for i in range(count):
                    total = total + pool[h, i].astype(F32)
                centre = total / count
                square = jnp.zeros((piece, width), F32)
                for i in range(count):
                    dev = pool[h, i].astype(F32) - centre
                    square = square + dev * dev
                result[h, col, 0] = centre.astype(BF16)
                result[h, col, 1] = jnp.sqrt(square / count).astype(BF16)
                for d in range(peers - 1):
                    res_to(d, h).start()
        all_fin = pool.at[:, pl.ds(0, members * (peers - 1))]
        three = result.at[:, pl.ds(0, peers - 1)]
        with jax.named_scope("t3_reswait"):
            pltpu.make_async_copy(all_fin, all_fin, fin_ssem).wait()
            pltpu.make_async_copy(three, three, res_rsem).wait()
        with jax.named_scope("t4_out"):
            for x in range(peers):
                for h in range(PIECES):
                    at = slice(x * rows + h * piece, x * rows + (h + 1) * piece)
                    both_ref[0, at, :] = result[h, x, 0]
                    both_ref[1, at, :] = result[h, x, 1]
            pltpu.make_async_copy(three, three, res_ssem).wait()

    return kernel


def local(node_latents, edge_latents, neighbours, edge_source, edge_dest, edge_count,
          edge_in, edge_out, node_in, node_out, biases, gains):
    members, blk, width = node_latents.shape
    slots = edge_source.shape[1]
    nbrs = neighbours.shape[1]
    groups = lax.axis_size("graph")
    peers = lax.axis_size("member")
    near = len(OFFSETS)
    halo = near * CAP
    rows = blk // peers
    piece = rows // PIECES
    vm = pltpu.VMEM
    dma = pltpu.SemaphoreType.DMA
    scratch = [
        vm((members * blk, width), BF16), vm((slots, width), BF16), vm((3, width, width), BF16),
        vm((width, width), BF16), vm((2, width, width), BF16), vm((width, width), BF16),
        vm((4, width), F32), vm((2, width), F32),
        vm((1, slots), jnp.int32), vm((1, slots), jnp.int32),
        pltpu.SMEM((1, nbrs), jnp.int32),
        vm((near, 8, blk), F32), vm((near, 8, blk), F32),
        vm((members, 2 * blk, width), BF16), vm((members, 2 * blk, width), BF16), vm((members, halo, width), BF16),
        vm((slots, 2 * blk), BF16), vm((slots, 2 * blk), BF16), vm((slots, width), F32), vm((members, slots, width), F32), vm((members * blk, width), F32),
        vm((blk, slots), BF16), vm((members, blk, width), BF16), vm((PIECES, members * peers, piece, width), BF16),
        vm((PIECES, peers, 2, piece, width), BF16),
        dma((14,)), dma((2,)), dma(()), dma((members,)), dma(()), dma((PIECES,)), dma(()), dma(()),
    ]
    out = jax.ShapeDtypeStruct((blk, width), BF16)
    args = [node_latents.reshape(members * blk, width), edge_latents, neighbours, edge_source, edge_dest, edge_count,
            edge_in, edge_out, node_in, node_out, biases, gains]
    specs = [pl.BlockSpec(memory_space=pltpu.HBM)] * len(args)
    specs[5] = pl.BlockSpec(memory_space=pltpu.SMEM)
    args = [a if i == 5 else pltpu.with_memory_space_constraint(a, pltpu.HBM) for i, a in enumerate(args)]
    both = pl.pallas_call(
        make_kernel(groups, peers, members, blk, slots, width, nbrs),
        out_shape=jax.ShapeDtypeStruct((2, blk, width), BF16),
        in_specs=specs,
        out_specs=pl.BlockSpec(memory_space=pltpu.VMEM),
        scratch_shapes=scratch,
        compiler_params=pltpu.CompilerParams(
            collective_id=0, has_side_effects=True, vmem_limit_bytes=52 * 1024 * 1024
        ),
    )(*args)
    return both[0], both[1]


def solution(mesh):
    return jax.shard_map(
        local,
        mesh=mesh,
        in_specs=(
            P("member", "graph", None), P("graph", None), P("graph", None), P("graph", None),
            P("graph", None), P("graph"), P(), P(), P(), P(), P(), P(),
        ),
        out_specs=(P("graph", None), P("graph", None)),
        check_vma=False,
    )
```

time: 45.5 us -> 42.8 us (0.941)
  the two profiles are of different devices: /device:TPU:8 before, /device:TPU:2 now
where the time goes in v3:
time: 42.8 us; the launch traced here: 42.6 us
  Pallas kernels  40.6 us (95%)
  between operations  1.29 us (3%)
  local copies, waits for them, and re-layouts  0.72 us (2%)
    pallas_call x1, Pallas kernels, local(): pl.pallas_call(make_kernel(groups, peers, members, blk, slots, width, nbr...  40.6 us

profile of v3, /device:TPU:2, one launch (start us, length us, event | category | flops | bytes accessed | tf_op | source)
XLA Modules:
  0.0 42.6 jit_solution(1519229407032438542)
XLA Ops:
  1.3 40.6 %shard_map.131 = bf16[2,128,512]{2,1,0:T(8,128)(2,1)S(1)} custom-call(bf16[512,512]{1,0:T(8,128)(2,1)} %bitcast.5, bf16[768,512]{1,0:T(8,128)(2,1)} %edge_hbm.1, s32[1,4]{1,0:T(1,128)} %nbr_hbm.1, s32[1,768]{1,0:T(1,128)} %src_hbm.1, s32[1,768]{1,0:T(1,128)} %dst_hbm.1, s32[1]{0:T(128)S(6)} %copy.14.cnt_ref, bf16[1,3,512,512]{3,2,1,0:T(8,128)(2,1)} %win_hbm.1, ...), custom_call_target="tpu_custom_call" | custom-call | tf_op jit(solution)/shard_map/pallas_call | solution.py:307
  41.9 0.7 %slice_bitcast_fusion = (bf16[128,512]{1,0:T(8,128)(2,1)}, bf16[128,512]{1,0:T(8,128)(2,1)}) fusion(bf16[2,128,512]{2,1,0:T(8,128)(2,1)S(1)} %shard_map.131), kind=kLoop, calls=%fused_computation | loop fusion | bytes 524288 | tf_op jit(solution)/shard_map/squeeze | solution.py:317

commit v4 on v3

--- a/solution.py
+++ b/solution.py
@@ -9,6 +9,7 @@
 CAP = 32
 EPS = 1e-05
 PIECES = 2
+RELAY = 15
 MESH = pl.DeviceIdType.MESH
 F32 = jnp.float32
 BF16 = jnp.bfloat16
@@ -48,8 +49,8 @@
         both_ref,
         node_v, edge_v, win_v, wout_v, nin_v, nout_v, bias_v, gain_v,
         src_v, dst_v, nbr_s,
-        ask_out, ask_in, own, halo_in, outbox, hot, far_hot, eproj, pre, nproj, dhot, fin, pool, result,
-        in_sems, ask_sems, row_ssem, row_rsem, fin_ssem, fin_rsem, res_ssem, res_rsem,
+        ask_out, ask_in, relay_in, own, halo_in, outbox, hot, far_hot, eproj, pre, nproj, dhot, fin, pool, result,
+        in_sems, ask_ssem, ask_rsem, relay_ssem, relay_rsem, row_ssem, row_rsem, fin_ssem, fin_rsem, res_ssem, res_rsem,
     ):
         me = lax.axis_index("graph")
         col = lax.axis_index("member")
@@ -70,11 +71,28 @@
         copies = [load(i, s, d) for i, (s, d) in enumerate(loads)]
         for c in copies[:2]:
             c.start()
+        is_first, is_last, is_relay = me < RADIUS, me >= groups - RADIUS, me == RELAY
+
         barrier = pltpu.get_barrier_semaphore()
-        for g in near_ids:
-            pl.semaphore_signal(barrier, inc=1, device_id={"graph": g, "member": col}, device_id_type=MESH)
+
+        def greet(g, x):
+            pl.semaphore_signal(barrier, inc=1, device_id={"graph": g, "member": x}, device_id_type=MESH)
+
+        pl.when(is_last)(lambda: greet(RELAY, col))
+        for p in FAR_FIRST:
+            if OFFSETS[p] > 0:
+                greet(back_ids[p], col)
+            else:
+                pl.when(me - OFFSETS[p] < groups)(lambda p=p: greet(back_ids[p], col))
         for x in peer_ids:
-            pl.semaphore_signal(barrier, inc=1, device_id={"graph": me, "member": x}, device_id_type=MESH)
+            greet(me, x)
+
+        @pl.when(is_relay)
+        def _():
+            for e in range(RADIUS):
+                greet(e, col)
+
+        expected = near + peers - 1 + jnp.where(is_first, 1 + me - RADIUS, 0) + jnp.where(is_relay, RADIUS, 0)
         for c in copies[2:]:
             c.start()
 
@@ -109,15 +127,39 @@
             ).astype(BF16)
 
         with jax.named_scope("s03_barrier"):
-            pl.semaphore_wait(barrier, near + peers - 1)
+            pl.semaphore_wait(barrier, expected)
 
         def ask(p):
             return pltpu.make_async_remote_copy(
-                src_ref=ask_out.at[p], dst_ref=ask_in.at[p], send_sem=ask_sems.at[0], recv_sem=ask_sems.at[1],
+                src_ref=ask_out.at[p], dst_ref=ask_in.at[p], send_sem=ask_ssem, recv_sem=ask_rsem.at[p // RADIUS],
                 device_id={"graph": near_ids[p], "member": col}, device_id_type=MESH)
 
+        def ask_relay(p):
+            return pltpu.make_async_remote_copy(
+                src_ref=ask_out.at[p], dst_ref=relay_in.at[me * RADIUS + p - RADIUS],
+                send_sem=ask_ssem, recv_sem=relay_rsem,
+                device_id={"graph": RELAY, "member": col}, device_id_type=MESH)
+
+        def forward(e, o):
+            return pltpu.make_async_remote_copy(
+                src_ref=relay_in.at[e * RADIUS + o - 1], dst_ref=ask_in.at[RADIUS + o - 1],
+                send_sem=relay_ssem, recv_sem=ask_rsem.at[1],
+                device_id={"graph": groups + e - o, "member": col}, device_id_type=MESH)
+
         for p in FAR_FIRST:
-            ask(p).start()
+            if OFFSETS[p] > 0:
+                ask(p).start()
+            else:
+                pl.when(me + OFFSETS[p] >= 0)(lambda p=p: ask(p).start())
+                pl.when(me + OFFSETS[p] < 0)(lambda p=p: ask_relay(p).start())
+
+        @pl.when(is_relay)
+        def _():
+            with jax.named_scope("s035_relay"):
+                pltpu.make_async_copy(ask_out, ask_out, relay_rsem).wait()
+                for e in range(RADIUS):
+                    for o in range(e + 1, RADIUS + 1):
+                        forward(e, o).start()
 
         with jax.named_scope("s04_project"):
             for c in copies[2:5]:
@@ -148,9 +190,6 @@
                 far_hot[part, :] = jnp.where(place_c == near_of, pick, 0.0).astype(BF16)
             dhot[...] = jnp.where((subn == dst) & live, 1.0, 0.0).astype(BF16)
 
-        with jax.named_scope("s06_askwait"):
-            pltpu.make_async_copy(ask_in, ask_in, ask_sems.at[1]).wait()
-
         def rows_to(m, p):
             return pltpu.make_async_remote_copy(
                 src_ref=outbox.at[m, pl.ds(p * CAP, CAP), :],
@@ -158,41 +197,52 @@
                 send_sem=row_ssem, recv_sem=row_rsem.at[m],
                 device_id={"graph": back_ids[p], "member": col}, device_id_type=MESH)
 
-        with jax.named_scope("s07_select"):
-            theirs = jnp.concatenate(
-                [jnp.where(capf == ask_in[p, 0:1, :], 1.0, 0.0) for p in range(near)], axis=0
-            ).astype(BF16)
-
-            def select(m, carry):
-                outbox[m] = dot_nn(theirs, own[m, 0:blk, :]).astype(BF16)
-                for p in FAR_FIRST:
-                    rows_to(m, p).start()
-                return carry
-
-            lax.fori_loop(0, members, select, 0)
-
-        with jax.named_scope("s08_recv"):
-            for c in copies[5:8]:
-                c.wait()
-            part = (0.5 * dot_nn(node_v[...], win_v[2])).astype(BF16)
-            for m in range(members):
-                own[m, blk : 2 * blk, :] = part[m * blk : (m + 1) * blk, :]
-                halo_in[m, halo:, :] = jnp.zeros((2 * blk - halo, width), BF16)
-        with jax.named_scope("s09_eproj"):
-            for c in copies[8:10]:
-                c.wait()
-            eproj[...] = 0.5 * (dot_nn(edge_v[...], win_v[0]) + bias_v[0:1, :])
-        with jax.named_scope("s10_pre"):
-
-            def precompute(m, carry):
-                pre[m] = eproj[...] + dot_nn(hot[...], own[m])
-                return carry
-
-            lax.fori_loop(0, members, precompute, 0)
-        with jax.named_scope("s11_nodes"):
-            for c in copies[10:]:
-                c.wait()
-            nproj[...] = 0.5 * (dot_nn(node_v[...], nin_v[0]) + bias_v[2:3, :])
+        def serve(side):
+            first = side * RADIUS
+            with jax.named_scope("s06_askwait"):
+                asks = ask_in.at[pl.ds(first, RADIUS)]
+                pltpu.make_async_copy(asks, asks, ask_rsem.at[side]).wait()
+            with jax.named_scope("s07_select"):
+                theirs = jnp.concatenate(
+                    [jnp.where(capf == ask_in[p, 0:1, :], 1.0, 0.0) for p in range(first, first + RADIUS)], axis=0
+                ).astype(BF16)
+
+                def select(m, carry):
+                    outbox[m, first * CAP : (first + RADIUS) * CAP, :] = dot_nn(theirs, own[m, 0:blk, :]).astype(BF16)
+                    for p in reversed(range(first, first + RADIUS)):
+                        rows_to(m, p).start()
+                    return carry
+
+                lax.fori_loop(0, members, select, 0)
+
+        def local_work():
+            with jax.named_scope("s08_recv"):
+                for c in copies[5:8]:
+                    c.wait()
+                part = (0.5 * dot_nn(node_v[...], win_v[2])).astype(BF16)
+                for m in range(members):
+                    own[m, blk : 2 * blk, :] = part[m * blk : (m + 1) * blk, :]
+                    halo_in[m, halo:, :] = jnp.zeros((2 * blk - halo, width), BF16)
+            with jax.named_scope("s09_eproj"):
+                for c in copies[8:10]:
+                    c.wait()
+                eproj[...] = 0.5 * (dot_nn(edge_v[...], win_v[0]) + bias_v[0:1, :])
+            with jax.named_scope("s10_pre"):
+
+                def precompute(m, carry):
+                    pre[m] = eproj[...] + dot_nn(hot[...], own[m])
+                    return carry
+
+                lax.fori_loop(0, members, precompute, 0)
+            with jax.named_scope("s11_nodes"):
+                for c in copies[10:]:
+                    c.wait()
+                nproj[...] = 0.5 * (dot_nn(node_v[...], nin_v[0]) + bias_v[2:3, :])
+
+        serve(1)
+        pl.when(is_first)(local_work)
+        serve(0)
+        pl.when(me >= RADIUS)(local_work)
 
         def fin_to(m, d, h):
             at = pl.multiple_of(peer_ids[d] * rows + h * piece, piece)
@@ -229,7 +279,12 @@
         lax.fori_loop(0, members, one_member, 0)
 
         with jax.named_scope("t0_drain"):
-            pltpu.make_async_copy(ask_out, ask_out, ask_sems.at[0]).wait()
+            pltpu.make_async_copy(ask_out, ask_out, ask_ssem).wait()
+
+            @pl.when(is_relay)
+            def _():
+                pltpu.make_async_copy(ask_out, ask_out, relay_ssem).wait()
+
             pltpu.make_async_copy(outbox, outbox, row_ssem).wait()
 
         def res_to(d, h):
@@ -291,12 +346,12 @@
         vm((4, width), F32), vm((2, width), F32),
         vm((1, slots), jnp.int32), vm((1, slots), jnp.int32),
         pltpu.SMEM((1, nbrs), jnp.int32),
-        vm((near, 8, blk), F32), vm((near, 8, blk), F32),
+        vm((near, 8, blk), F32), vm((near, 8, blk), F32), vm((RADIUS * RADIUS, 8, blk), F32),
         vm((members, 2 * blk, width), BF16), vm((members, 2 * blk, width), BF16), vm((members, halo, width), BF16),
         vm((slots, 2 * blk), BF16), vm((slots, 2 * blk), BF16), vm((slots, width), F32), vm((members, slots, width), F32), vm((members * blk, width), F32),
         vm((blk, slots), BF16), vm((members, blk, width), BF16), vm((PIECES, members * peers, piece, width), BF16),
         vm((PIECES, peers, 2, piece, width), BF16),
-        dma((14,)), dma((2,)), dma(()), dma((members,)), dma(()), dma((PIECES,)), dma(()), dma(()),
+        dma((14,)), dma(()), dma((2,)), dma(()), dma(()), dma(()), dma((members,)), dma(()), dma((PIECES,)), dma(()), dma(()),
     ]
     out = jax.ShapeDtypeStruct((blk, width), BF16)
     args = [node_latents.reshape(members * blk, width), edge_latents, neighbours, edge_source, edge_dest, edge_count,

time: 42.8 us -> 39.8 us (0.930)
  Pallas kernels: 40.6 us -> 37.7 us
    pallas_call x1, Pallas kernels: 40.6 us -> 37.7 us  [local(): pl.pallas_call(make_kernel(groups, peers, members, blk, slots, width, nbr...]
where the time goes in v4:
time: 39.8 us; the launch traced here: 39.7 us
  Pallas kernels  37.7 us (95%)
  between operations  1.29 us (3%)
  local copies, waits for them, and re-layouts  0.72 us (2%)
    pallas_call x1, Pallas kernels, local(): pl.pallas_call(make_kernel(groups, peers, members, blk, slots, width, nbr...  37.7 us

profile of v4, /device:TPU:2, one launch (start us, length us, event | category | flops | bytes accessed | tf_op | source)
XLA Modules:
  0.0 39.7 jit_solution(5883300392421161867)
XLA Ops:
  1.3 37.7 %shard_map.131 = bf16[2,128,512]{2,1,0:T(8,128)(2,1)S(1)} custom-call(bf16[512,512]{1,0:T(8,128)(2,1)} %bitcast.5, bf16[768,512]{1,0:T(8,128)(2,1)} %edge_hbm.1, s32[1,4]{1,0:T(1,128)} %nbr_hbm.1, s32[1,768]{1,0:T(1,128)} %src_hbm.1, s32[1,768]{1,0:T(1,128)} %dst_hbm.1, s32[1]{0:T(128)S(6)} %copy.14.cnt_ref, bf16[1,3,512,512]{3,2,1,0:T(8,128)(2,1)} %win_hbm.1, ...), custom_call_target="tpu_custom_call" | custom-call | tf_op jit(solution)/shard_map/pallas_call | solution.py:362
  39.0 0.7 %slice_bitcast_fusion = (bf16[128,512]{1,0:T(8,128)(2,1)}, bf16[128,512]{1,0:T(8,128)(2,1)}) fusion(bf16[2,128,512]{2,1,0:T(8,128)(2,1)S(1)} %shard_map.131), kind=kLoop, calls=%fused_computation | loop fusion | bytes 524288 | tf_op jit(solution)/shard_map/squeeze | solution.py:372
